TPU v7x, 32 devices: a 4x2x2 block of a 4x4x8 slice. The times are simulated.
32 devices in a mesh: dp: 4 (over y, z), ep: 8 (over x, core).
Axes of the slice: x: 4, y: 2, z: 2, core: 2. Of those that a mesh axis runs over, the one named last changes fastest.
The devices are a block of a 4x4x8 slice.
Arguments:
- tokens: bfloat16 [64, 256, 1024], P(('dp', 'ep')), parts along dimension 0
- attn_gain_1: bfloat16 [1024], replicated
- w_query_1: bfloat16 [1024, 8, 128], replicated
- w_key_1: bfloat16 [1024, 2, 128], replicated
- w_value_1: bfloat16 [1024, 2, 128], replicated
- w_out_1: bfloat16 [8, 128, 1024], replicated
- moe_gain_1: bfloat16 [1024], replicated
- w_router_1: bfloat16 [1024, 16], replicated
- routes_1: int32 [64, 256, 4], P(('dp', 'ep')), parts along dimension 0
- w_gate_1: bfloat16 [16, 1024, 1792], P('ep')
- w_up_1: bfloat16 [16, 1024, 1792], P('ep')
- w_down_1: bfloat16 [16, 1792, 1024], P('ep')
- shared_gate_1: bfloat16 [1024, 1792], replicated
- shared_up_1: bfloat16 [1024, 1792], replicated
- shared_down_1: bfloat16 [1792, 1024], replicated
- attn_gain_2: bfloat16 [1024], replicated
- w_query_2: bfloat16 [1024, 8, 128], replicated
- w_key_2: bfloat16 [1024, 2, 128], replicated
- w_value_2: bfloat16 [1024, 2, 128], replicated
- w_out_2: bfloat16 [8, 128, 1024], replicated
- moe_gain_2: bfloat16 [1024], replicated
- w_router_2: bfloat16 [1024, 16], replicated
- routes_2: int32 [64, 256, 4], P(('dp', 'ep')), parts along dimension 0
- w_gate_2: bfloat16 [16, 1024, 1792], P('ep')
- w_up_2: bfloat16 [16, 1024, 1792], P('ep')
- w_down_2: bfloat16 [16, 1792, 1024], P('ep')
- shared_gate_2: bfloat16 [1024, 1792], replicated
- shared_up_2: bfloat16 [1024, 1792], replicated
- shared_down_2: bfloat16 [1792, 1024], replicated
Outputs:
- output: bfloat16 [64, 256, 1024], P(('dp', 'ep')), parts along dimension 0
There are 4 independent parts. A program takes and returns all parts, laid end to end along the dimension named above; an argument that names none is the same for every part.
All inputs are finite; a program needn't handle non-finite values.
Results may differ from a plain program's by a relative error of at most 0.02.
Values are sent between devices in bfloat16 or wider.
A program may use at most 768 MiB of HBM per device.

v0:
```python
import jax
import jax.numpy as jnp
from jax import lax
from jax.sharding import PartitionSpec as P

NORM_EPS = 1e-6


def rms_norm(hidden, gain):
    hidden_f32 = hidden.astype(jnp.float32)
    inv_rms = lax.rsqrt(jnp.mean(hidden_f32 * hidden_f32, axis=-1, keepdims=True) + NORM_EPS)
    return (hidden_f32 * inv_rms * gain.astype(jnp.float32)).astype(jnp.bfloat16)


def attention_block(hidden, gain, w_query, w_key, w_value, w_out):
    batch, seq_len, model_dim = hidden.shape
    heads, head_dim = w_query.shape[1], w_query.shape[2]
    kv_heads = w_key.shape[1]
    group = heads // kv_heads
    normed = rms_norm(hidden, gain)
    query = jnp.einsum('bsd,dnh->bsnh', normed, w_query, preferred_element_type=jnp.float32).astype(jnp.bfloat16)
    query = query.reshape(batch, seq_len, kv_heads, group, head_dim)
    key_proj = jnp.einsum('bsd,dkh->bskh', normed, w_key, preferred_element_type=jnp.float32).astype(jnp.bfloat16)
    value = jnp.einsum('bsd,dkh->bskh', normed, w_value, preferred_element_type=jnp.float32).astype(jnp.bfloat16)
    scores = jnp.einsum('bskgh,btkh->bkgst', query, key_proj, preferred_element_type=jnp.float32) * (head_dim ** -0.5)
    causal = lax.broadcasted_iota(jnp.int32, (seq_len, seq_len), 0) >= lax.broadcasted_iota(jnp.int32, (seq_len, seq_len), 1)
    attn_probs = jax.nn.softmax(jnp.where(causal, scores, -1e30), axis=-1).astype(jnp.bfloat16)
    mixed = jnp.einsum('bkgst,btkh->bskgh', attn_probs, value, preferred_element_type=jnp.float32).astype(jnp.bfloat16)
    out_heads = w_out.reshape(kv_heads, group, head_dim, model_dim)
    projected = jnp.einsum('bskgh,kghd->bsd', mixed, out_heads, preferred_element_type=jnp.float32)
    return (hidden.astype(jnp.float32) + projected).astype(jnp.bfloat16)


def dispatch_plan(choices, num_experts, capacity):
    tokens, top_k = choices.shape
    num_rows = tokens * top_k
    flat_ids = choices.reshape(num_rows)
    order = jnp.argsort(flat_ids, stable=True)
    sorted_ids = flat_ids[order]
    expert_ids = jnp.arange(num_experts, dtype=flat_ids.dtype)
    starts = jnp.searchsorted(sorted_ids, expert_ids, side='left').astype(jnp.int32)
    ends = jnp.searchsorted(sorted_ids, expert_ids, side='right').astype(jnp.int32)
    slot_src = starts[:, None] + jnp.arange(capacity, dtype=jnp.int32)[None, :]
    slot_used = slot_src < ends[:, None]
    slot_token = order[jnp.minimum(slot_src, num_rows - 1)] // top_k
    rank = jnp.zeros((num_rows,), jnp.int32).at[order].set(jnp.arange(num_rows, dtype=jnp.int32))
    row_loc = flat_ids * capacity + rank - starts[flat_ids]
    return slot_token, slot_used, row_loc.reshape(tokens, top_k)


def expert_ffn(rows, w_gate, w_up, w_down):
    gate_act = jnp.einsum('secd,edf->secf', rows, w_gate, preferred_element_type=jnp.float32)
    up_act = jnp.einsum('secd,edf->secf', rows, w_up, preferred_element_type=jnp.float32)
    hidden_act = (jax.nn.silu(gate_act) * up_act).astype(jnp.bfloat16)
    return jnp.einsum('secf,efd->secd', hidden_act, w_down, preferred_element_type=jnp.float32).astype(jnp.bfloat16)


def shared_ffn(normed, shared_gate, shared_up, shared_down):
    gate_act = jnp.dot(normed, shared_gate, preferred_element_type=jnp.float32)
    up_act = jnp.dot(normed, shared_up, preferred_element_type=jnp.float32)
    hidden_act = (jax.nn.silu(gate_act) * up_act).astype(jnp.bfloat16)
    return jnp.dot(hidden_act, shared_down, preferred_element_type=jnp.float32)


def moe_layer(hidden, layer_params, ep_size):
    (attn_gain, w_query, w_key, w_value, w_out, moe_gain, w_router, routes, w_gate, w_up, w_down, shared_gate, shared_up, shared_down) = layer_params
    batch, seq_len, model_dim = hidden.shape
    tokens = batch * seq_len
    local_count = w_gate.shape[0]
    num_experts = local_count * ep_size
    top_k = routes.shape[-1]
    capacity = 3 * tokens * top_k // num_experts
    residual = attention_block(hidden, attn_gain, w_query, w_key, w_value, w_out).reshape(tokens, model_dim)
    normed = rms_norm(residual, moe_gain)
    choices = routes.reshape(tokens, top_k)
    logits = jnp.dot(normed, w_router, preferred_element_type=jnp.float32)
    gates = jax.nn.softmax(jnp.take_along_axis(logits, choices, axis=1), axis=-1)
    slot_token, slot_used, row_loc = dispatch_plan(choices, num_experts, capacity)
    send = jnp.where(slot_used[:, :, None], normed[slot_token], jnp.zeros((), jnp.bfloat16))
    send = send.reshape(ep_size, local_count, capacity, model_dim)
    received = lax.all_to_all(send, 'ep', 0, 0, tiled=True)
    expert_out = expert_ffn(received, w_gate, w_up, w_down)
    returned = lax.all_to_all(expert_out, 'ep', 0, 0, tiled=True)
    picked = returned.reshape(num_experts * capacity, model_dim)[row_loc]
    routed = jnp.sum(gates[:, :, None] * picked.astype(jnp.float32), axis=1)
    shared = shared_ffn(normed, shared_gate, shared_up, shared_down)
    layer_out = (residual.astype(jnp.float32) + routed + shared).astype(jnp.bfloat16)
    return layer_out.reshape(batch, seq_len, model_dim)


def solution(mesh):
    ep_size = mesh.shape['ep']
    token_spec = P(('dp', 'ep'))
    layer_specs = (P(), P(), P(), P(), P(), P(), P(), token_spec, P('ep'), P('ep'), P('ep'), P(), P(), P())
    in_specs = (token_spec,) + layer_specs + layer_specs

    def local_step(tokens, *params):
        hidden = tokens
        for layer in range(2):
            hidden = moe_layer(hidden, params[14 * layer:14 * layer + 14], ep_size)
        return hidden

    return jax.shard_map(local_step, mesh=mesh, in_specs=in_specs, out_specs=token_spec, check_vma=False)
```

profile of v0, /device:TPU:81, one launch (start us, length us, event | category | flops | bytes accessed | tf_op | source)
XLA Modules:
  0.0 1061.7 jit_solution(18418479753580389856)
XLA Ops:
  6.8 11.8 %gather_fusion.4 = s32[2048]{0:T(1024)S(1)} fusion(s32[2048]{0:T(1024)S(1)} %reshape_reshape.10, s32[2048]{0:T(1024)S(1)} %get-tuple-element.391), kind=kCustom, calls=%fused_computation.6 | custom fusion | bytes 24576 | tf_op jit(solution)/shard_map/gather | solution.py:39
  18.5 8.5 while.74
  49.0 34.3 %gather_fusion.5 = s32[6144]{0:T(1024)S(1)} fusion(s32[2048]{0:T(1024)S(1)} %get-tuple-element.248, s32[6144]{0:T(1024)S(1)} %broadcast_clamp_fusion.3), kind=kCustom, calls=%fused_computation.7 | custom fusion | bytes 73728 | tf_op jit(solution)/shard_map/gather | solution.py:45
  83.4 8.5 while.75
  92.3 26.8 %gather_fusion.6 = bf16[6144,1024]{1,0:T(8,128)(2,1)} fusion(bf16[512,1024]{1,0:T(8,128)(2,1)S(1)} %fusion.89, s32[6144]{0:T(1024)S(1)} %broadcast_clamp_fusion.1), kind=kCustom, calls=%fused_computation.8 | custom fusion | bytes 25190400 | tf_op jit(solution)/shard_map/gather | solution.py:79
  119.3 10.7 %broadcast_select_fusion.9 = bf16[8,2,384,1024]{3,2,1,0:T(8,128)(2,1)} fusion(bf16[8,2,384,1024]{3,2,1,0:T(8,128)(2,1)} %bitcast.345, pred[8,2,384]{2,1,0:T(4,128)(4,1)S(1)} %add_compare_fusion.1), kind=kLoop, calls=%fused_computation.71 | loop fusion | flops 6291456 | bytes 25171968 | tf_op jit(solution)/shard_map/jit(_where)/select_n | solution.py:79
  144.2 20.5 %gather_fusion.8 = s32[2048]{0:T(1024)} fusion(s32[2048]{0:T(1024)S(1)} %reshape_reshape.12, s32[2048]{0:T(1024)S(1)} %get-tuple-element.389), kind=kCustom, calls=%fused_computation.10 | custom fusion | bytes 24576 | tf_op jit(solution)/shard_map/gather | solution.py:39
  164.8 111.3 %all-to-all-done = bf16[8,2,384,1024]{3,2,1,0:T(8,128)(2,1)} async-done(((bf16[8,2,384,1024]{3,2,1,0:T(8,128)(2,1)}), bf16[8,2,384,1024]{3,2,1,0:T(8,128)(2,1)}, u32[]{:S(2)}, u32[]{:S(2)}) %all-to-all-start) | async-done | bytes 12582944 | tf_op jit(solution)/shard_map/all_to_all | solution.py:81
  276.1 31.7 %fusion.40 = f32[2,8,384,1792]{3,2,1,0:T(8,128)} fusion(bf16[8,2,384,1024]{3,2,1,0:T(8,128)(2,1)} %all-to-all-done, bf16[2,1024,1792]{2,1,0:T(8,128)(2,1)} %param.48), kind=kOutput, calls=%fused_computation.76 | convolution fusion | flops 22548578304 | bytes 63963136 | tf_op jit(solution)/shard_map/secd,edf->secf/dot_general | solution.py:52
  307.8 35.6 %fusion.221 = bf16[8,2,384,1792]{3,2,0,1:T(8,128)(2,1)} fusion(f32[2,8,384,1792]{3,2,1,0:T(8,128)} %fusion.40, bf16[8,2,384,1024]{3,2,1,0:T(8,128)(2,1)} %all-to-all-done, bf16[2,1024,1792]{2,1,0:T(8,128)(2,1)} %param.49), kind=kOutput, calls=%fused_computation.58.clone.clone.clone.clone | convolution fusion | flops 22614638592 | bytes 85983232 | tf_op jit(solution)/shard_map/secd,edf->secf/dot_general | solution.py:53
  343.4 28.4 %convert_bitcast_fusion.1 = bf16[8,2,384,1024]{3,2,0,1:T(8,128)(2,1)S(1)} fusion(bf16[2,1792,1024]{2,1,0:T(8,128)(2,1)} %param.50, bf16[8,2,384,1792]{3,2,0,1:T(8,128)(2,1)} %fusion.221), kind=kOutput, calls=%fused_computation.69 | convolution fusion | flops 22554869760 | bytes 41943040 | tf_op jit(solution)/shard_map/secf,efd->secd/dot_general | solution.py:55
  383.7 8.5 while.76
  392.5 8.2 scatter_custom_fusion
  412.8 16.8 %gather_fusion.12 = f32[2048]{0:T(1024)S(1)} fusion(f32[512,16]{0,1:T(8,128)S(1)} %fusion.183, s32[2048]{0:T(1024)S(1)} %reshape.837), kind=kCustom, calls=%fused_computation.clone | custom fusion | bytes 32768 | tf_op jit(solution)/shard_map/jit(take_along_axis)/gather | solution.py:77
  430.4 34.3 %gather_fusion.9 = s32[6144]{0:T(1024)S(1)} fusion(s32[2048]{0:T(1024)S(1)} %copy-done.3, s32[6144]{0:T(1024)S(1)} %broadcast_clamp_fusion.2), kind=kCustom, calls=%fused_computation.11 | custom fusion | bytes 73728 | tf_op jit(solution)/shard_map/gather | solution.py:45
  464.8 8.5 while.77
  479.5 42.7 %all-to-all-done.1 = bf16[8,2,384,1024]{3,2,1,0:T(8,128)(2,1)} async-done(((bf16[8,2,384,1024]{3,2,1,0:T(8,128)(2,1)}), bf16[8,2,384,1024]{3,2,1,0:T(8,128)(2,1)}, u32[]{:S(2)}, u32[]{:S(2)}) %all-to-all-start.1) | async-done | bytes 12582944 | tf_op jit(solution)/shard_map/all_to_all | solution.py:83
  522.2 17.2 %gather_fusion.7 = bf16[2048,1024]{1,0:T(8,128)(2,1)} fusion(bf16[6144,1024]{1,0:T(8,128)(2,1)} %bitcast.29, s32[2048]{0:T(1024)S(1)} %broadcast_clamp_fusion.5), kind=kCustom, calls=%fused_computation.9 | custom fusion | bytes 8396800 | tf_op jit(solution)/shard_map/gather | solution.py:84
  539.4 8.7 reshape.732
  548.1 10.1 multiply_reduce_fusion.1
  558.2 9.3 multiply_reduce_fusion.2
  592.9 26.9 %gather_fusion.10 = bf16[6144,1024]{1,0:T(8,128)(2,1)} fusion(bf16[512,1024]{1,0:T(8,128)(2,1)S(1)} %fusion.79, s32[6144]{0:T(1024)S(1)} %broadcast_clamp_fusion), kind=kCustom, calls=%fused_computation.12 | custom fusion | bytes 25190400 | tf_op jit(solution)/shard_map/gather | solution.py:79
  626.2 142.4 %all_to_all.20 = bf16[8,2,384,1024]{3,2,1,0:T(8,128)(2,1)S(1)} all-to-all(bf16[8,2,384,1024]{3,2,1,0:T(8,128)(2,1)S(1)} %broadcast_select_fusion.8), channel_id=1, replica_groups=mesh['dp'=4,'ep'=8] {'ep'}, dimensions={0} | all-to-all | bytes 25165824 | tf_op jit(solution)/shard_map/all_to_all | solution.py:81
  773.2 29.8 %fusion.36 = f32[2,8,384,1792]{3,2,1,0:T(8,128)} fusion(bf16[8,2,384,1024]{3,2,1,0:T(8,128)(2,1)S(1)} %all_to_all.20, bf16[2,1024,1792]{2,1,0:T(8,128)(2,1)} %param.62), kind=kOutput, calls=%fused_computation.73 | convolution fusion | flops 22548578304 | bytes 63963136 | tf_op jit(solution)/shard_map/secd,edf->secf/dot_general | solution.py:52
  803.0 35.6 %fusion.217 = bf16[8,2,384,1792]{3,2,0,1:T(8,128)(2,1)} fusion(f32[2,8,384,1792]{3,2,1,0:T(8,128)} %fusion.36, bf16[8,2,384,1024]{3,2,1,0:T(8,128)(2,1)} %copy-done.13, bf16[2,1024,1792]{2,1,0:T(8,128)(2,1)} %param.63), kind=kOutput, calls=%fused_computation.51.clone.clone.clone.clone.1 | convolution fusion | flops 22614638592 | bytes 85983232 | tf_op jit(solution)/shard_map/secd,edf->secf/dot_general | solution.py:53
  838.6 28.4 %convert_bitcast_fusion = bf16[8,2,384,1024]{3,2,0,1:T(8,128)(2,1)S(1)} fusion(bf16[2,1792,1024]{2,1,0:T(8,128)(2,1)} %param.64, bf16[8,2,384,1792]{3,2,0,1:T(8,128)(2,1)} %fusion.217), kind=kOutput, calls=%fused_computation.68 | convolution fusion | flops 22554869760 | bytes 41943040 | tf_op jit(solution)/shard_map/secf,efd->secd/dot_general | solution.py:55
  899.3 16.8 %gather_fusion.13 = f32[2048]{0:T(1024)S(1)} fusion(f32[512,16]{0,1:T(8,128)S(1)} %fusion.185, s32[2048]{0:T(1024)S(1)} %reshape.842), kind=kCustom, calls=%fused_computation.5.clone | custom fusion | bytes 32768 | tf_op jit(solution)/shard_map/jit(take_along_axis)/gather | solution.py:77
  922.6 94.8 %all-to-all-done.3 = bf16[8,2,384,1024]{3,2,1,0:T(8,128)(2,1)} async-done(((bf16[8,2,384,1024]{3,2,1,0:T(8,128)(2,1)}), bf16[8,2,384,1024]{3,2,1,0:T(8,128)(2,1)}, u32[]{:S(2)}, u32[]{:S(2)}) %all-to-all-start.3) | async-done | bytes 12582944 | tf_op jit(solution)/shard_map/all_to_all | solution.py:83
  1017.4 17.2 %gather_fusion.11 = bf16[2048,1024]{1,0:T(8,128)(2,1)} fusion(bf16[6144,1024]{1,0:T(8,128)(2,1)} %bitcast.77, s32[2048]{0:T(1024)S(1)} %broadcast_clamp_fusion.4), kind=kCustom, calls=%fused_computation.13 | custom fusion | bytes 8396800 | tf_op jit(solution)/shard_map/gather | solution.py:84
  1034.6 8.5 reshape.733
  1043.1 8.7 multiply_reduce_fusion
  1051.8 9.4 fusion.81
  (387 shorter events, 182.0 us)
Async XLA Ops:
  0.0 412.4 %copy-start = (bf16[1024,16]{0,1:T(8,128)(2,1)S(1)}, bf16[1024,16]{0,1:T(8,128)(2,1)}, u32[]{:S(2)}) copy-start(bf16[1024,16]{0,1:T(8,128)(2,1)} %param.46) | copy-start | bytes 98308
  0.0 34.0 %copy-start.29 = (pred[256,256]{0,1:T(8,128)(4,1)}, pred[256,256]{0,1:T(8,128)(4,1)S(1)}, u32[]{:S(2)}) copy-start(pred[256,256]{0,1:T(8,128)(4,1)S(1)} %iota_compare_fusion.4) | copy-start | bytes 196612
  1.1 17.4 %copy-start.10 = (s32[2048]{0:T(1024)}, s32[2048]{0:T(1024)S(1)}, u32[]{:S(2)}) copy-start(s32[2048]{0:T(1024)S(1)} %reshape_reshape.10) | copy-start | bytes 24580
  6.7 20.5 %copy-start.14 = (bf16[2,256,1024]{2,1,0:T(8,128)(2,1)S(1)}, bf16[2,256,1024]{2,1,0:T(8,128)(2,1)}, u32[]{:S(2)}) copy-start(bf16[2,256,1024]{2,1,0:T(8,128)(2,1)} %param.39) | copy-start | bytes 3145732
  6.8 20.8 %copy-start.34 = (bf16[1024]{0:T(1024)(128)(2,1)S(1)}, bf16[1024]{0:T(1024)(128)(2,1)}, u32[]{:S(2)}) copy-start(bf16[1024]{0:T(1024)(128)(2,1)} %param.40) | copy-start | bytes 6148
  34.0 7.1 copy-start.38
  48.9 43.1 %copy-start.19 = (bf16[2,256,1024]{2,1,0:T(8,128)(2,1)}, bf16[2,256,1024]{2,1,0:T(8,128)(2,1)S(1)}, u32[]{:S(2)}) copy-start(bf16[2,256,1024]{2,1,0:T(8,128)(2,1)S(1)} %get-tuple-element.427) | copy-start | bytes 3145732
  92.3 26.9 %copy-start.4 = (bf16[512,1024]{1,0:T(8,128)(2,1)}, bf16[512,1024]{1,0:T(8,128)(2,1)S(1)}, u32[]{:S(2)}) copy-start(bf16[512,1024]{1,0:T(8,128)(2,1)S(1)} %fusion.89) | copy-start | bytes 3145732
  130.0 7.7 copy-start.27
  130.0 146.1 %all-to-all-start = ((bf16[8,2,384,1024]{3,2,1,0:T(8,128)(2,1)}), bf16[8,2,384,1024]{3,2,1,0:T(8,128)(2,1)}, u32[]{:S(2)}, u32[]{:S(2)}) async-start(bf16[8,2,384,1024]{3,2,1,0:T(8,128)(2,1)} %broadcast_select_fusion.9), calls=%async_computation | async-start | bytes 25165824 | tf_op jit(solution)/shard_map/all_to_all | solution.py:81
  138.6 26.2 %copy-start.8 = (s32[2048]{0:T(1024)}, s32[2048]{0:T(1024)S(1)}, u32[]{:S(2)}) copy-start(s32[2048]{0:T(1024)S(1)} %reshape_reshape.12) | copy-start | bytes 24580
  143.6 21.1 %copy-start.2 = (s32[2048]{0:T(1024)}, s32[2048]{0:T(1024)S(1)}, u32[]{:S(2)}) copy-start(s32[2048]{0:T(1024)S(1)} %get-tuple-element.251) | copy-start | bytes 24580
  377.2 6.5 copy-start.31
  377.2 6.5 copy-start.32
  377.2 15.1 %copy-start.18 = (s32[2,256,4]{2,1,0:T(8,128)S(1)}, s32[2,256,4]{2,1,0:T(8,128)}, u32[]{:S(2)}) copy-start(s32[2,256,4]{2,1,0:T(8,128)} %copy-done.17) | copy-start | bytes 24580
  377.2 23.5 %copy-start.23 = (s32[16]{0:T(128)S(1)}, s32[16]{0:T(128)}, u32[]{:S(2)}) copy-start(s32[16]{0:T(128)} %copy-done.22) | copy-start | bytes 196
  377.2 28.9 %copy-start.11 = (s32[2048]{0:T(1024)S(1)}, s32[2048]{0:T(1024)}, u32[]{:S(2)}) copy-start(s32[2048]{0:T(1024)} %copy-done.10) | copy-start | bytes 24580
  377.2 145.0 %all-to-all-start.1 = ((bf16[8,2,384,1024]{3,2,1,0:T(8,128)(2,1)}), bf16[8,2,384,1024]{3,2,1,0:T(8,128)(2,1)}, u32[]{:S(2)}, u32[]{:S(2)}) async-start(bf16[8,2,384,1024]{3,2,1,0:T(8,128)(2,1)} %copy.73), calls=%async_computation.1 | async-start | bytes 25165824 | tf_op jit(solution)/shard_map/all_to_all | solution.py:83
  383.7 28.4 %copy-start.26 = (s32[2,256,4]{1,2,0:T(4,128)S(1)}, s32[2,256,4]{1,2,0:T(4,128)}, u32[]{:S(2)}) copy-start(s32[2,256,4]{1,2,0:T(4,128)} %param.47) | copy-start | bytes 24580
  383.7 28.7 %copy-start.5 = (bf16[512,1024]{1,0:T(8,128)(2,1)S(1)}, bf16[512,1024]{1,0:T(8,128)(2,1)}, u32[]{:S(2)}) copy-start(bf16[512,1024]{1,0:T(8,128)(2,1)} %copy-done.4) | copy-start | bytes 3145732
  412.8 17.4 %copy-start.36 = (bf16[1024]{0:T(1024)(128)(2,1)S(1)}, bf16[1024]{0:T(1024)(128)(2,1)}, u32[]{:S(2)}) copy-start(bf16[1024]{0:T(1024)(128)(2,1)} %param.54) | copy-start | bytes 6148
  412.8 17.4 %copy-start.37 = (bf16[1024]{0:T(1024)(128)(2,1)S(1)}, bf16[1024]{0:T(1024)(128)(2,1)}, u32[]{:S(2)}) copy-start(bf16[1024]{0:T(1024)(128)(2,1)} %param.59) | copy-start | bytes 6148
  430.2 34.5 %copy-start.24 = (s32[16]{0:T(128)}, s32[16]{0:T(128)S(1)}, u32[]{:S(2)}) copy-start(s32[16]{0:T(128)S(1)} %convert_element_type.205) | copy-start | bytes 196
  592.9 26.9 %copy-start.6 = (bf16[512,1024]{1,0:T(8,128)(2,1)}, bf16[512,1024]{1,0:T(8,128)(2,1)S(1)}, u32[]{:S(2)}) copy-start(bf16[512,1024]{1,0:T(8,128)(2,1)S(1)} %fusion.79) | copy-start | bytes 3145732
  872.4 6.5 copy-start.16
  872.4 6.7 copy-start.28
  872.4 15.2 %copy-start.25 = (s32[16]{0:T(128)S(1)}, s32[16]{0:T(128)}, u32[]{:S(2)}) copy-start(s32[16]{0:T(128)} %copy-done.24) | copy-start | bytes 196
  872.4 20.4 %copy-start.9 = (s32[2048]{0:T(1024)S(1)}, s32[2048]{0:T(1024)}, u32[]{:S(2)}) copy-start(s32[2048]{0:T(1024)} %copy-done.8) | copy-start | bytes 24580
  872.4 26.5 %copy-start.7 = (bf16[512,1024]{1,0:T(8,128)(2,1)S(1)}, bf16[512,1024]{1,0:T(8,128)(2,1)}, u32[]{:S(2)}) copy-start(bf16[512,1024]{1,0:T(8,128)(2,1)} %copy-done.6) | copy-start | bytes 3145732
  872.4 26.5 %copy-start.33 = (bf16[1024,16]{0,1:T(8,128)(2,1)S(1)}, bf16[1024,16]{0,1:T(8,128)(2,1)}, u32[]{:S(2)}) copy-start(bf16[1024,16]{0,1:T(8,128)(2,1)} %param.60) | copy-start | bytes 98308
  872.4 145.0 %all-to-all-start.3 = ((bf16[8,2,384,1024]{3,2,1,0:T(8,128)(2,1)}), bf16[8,2,384,1024]{3,2,1,0:T(8,128)(2,1)}, u32[]{:S(2)}, u32[]{:S(2)}) async-start(bf16[8,2,384,1024]{3,2,1,0:T(8,128)(2,1)} %copy.88), calls=%async_computation.3 | async-start | bytes 25165824 | tf_op jit(solution)/shard_map/all_to_all | solution.py:83
  1051.8 9.4 copy-start.1
  (10 other events, 34.3 us)
where the time goes:
time: 1070 us; the launch traced here: 1060 us
  local copies, waits for them, and re-layouts  311 us (29%)
  matrix products  252 us (24%)
  waiting for transfers between devices  249 us (23%)
  blocking collectives  142 us (13%)
  other arithmetic  84.9 us (8%)
  starting transfers between devices  20.6 us (2%)
    all_to_all x1, blocking collectives, moe_layer(): received = lax.all_to_all(send, 'ep', 0, 0, tiled=True)  142 us
    all_to_all x2, waiting for transfers between devices, moe_layer(): returned = lax.all_to_all(expert_out, 'ep', 0, 0, tiled=True)  137 us
    all_to_all x1, waiting for transfers between devices, moe_layer(): received = lax.all_to_all(send, 'ep', 0, 0, tiled=True)  111 us
    dot_general x2, matrix products, expert_ffn(): jnp.einsum('secd,edf->secf', rows, w_up, preferred_element_type=jnp.float32)  71.1 us
    gather x4, local copies, waits for them, and re-layouts, dispatch_plan(): slot_token = order[jnp.minimum(slot_src, num_rows - 1)] // top_k  68.6 us
    dot_general x2, matrix products, expert_ffn(): jnp.einsum('secd,edf->secf', rows, w_gate, preferred_element_type=jnp.flo...  61.5 us
    dot_general x2, matrix products, expert_ffn(): jnp.einsum('secf,efd->secd', hidden_act, w_down, preferred_element_type=j...  56.7 us
    gather x2, local copies, waits for them, and re-layouts, moe_layer(): normed[slot_token]  53.7 us
  transfers between devices with their start and end apart: 3, of which 3 were waited for; matrix products, arithmetic and copies ran while one was open for 16% of the time, Pallas kernels for 0%

commit v1 on v0

v1 whole, which is shorter than its diff:
```python
import functools

import jax
import jax.numpy as jnp
from jax import lax
from jax.experimental import pallas as pl
from jax.experimental.pallas import tpu as pltpu
from jax.sharding import PartitionSpec as P

NORM_EPS = 1e-6
MESH = pl.DeviceIdType.MESH
F32 = jnp.float32
BF16 = jnp.bfloat16

OWN0, OPP0, OPP1, LEFT1, RIGHT0, LEFT0, RIGHT1, OWN1 = range(8)
UNITS = 8
CHUNK = 256


def rms_norm(hidden, gain):
    hidden_f32 = hidden.astype(F32)
    inv_rms = lax.rsqrt(jnp.mean(hidden_f32 * hidden_f32, axis=-1, keepdims=True) + NORM_EPS)
    return (hidden_f32 * inv_rms * gain.astype(F32)).astype(BF16)


def attention_block(hidden, gain, w_query, w_key, w_value, w_out):
    batch, seq_len, model_dim = hidden.shape
    heads, head_dim = w_query.shape[1], w_query.shape[2]
    kv_heads = w_key.shape[1]
    group = heads // kv_heads
    normed = rms_norm(hidden, gain)
    query = jnp.einsum('bsd,dnh->bsnh', normed, w_query, preferred_element_type=F32).astype(BF16)
    query = query.reshape(batch, seq_len, kv_heads, group, head_dim)
    key_proj = jnp.einsum('bsd,dkh->bskh', normed, w_key, preferred_element_type=F32).astype(BF16)
    value = jnp.einsum('bsd,dkh->bskh', normed, w_value, preferred_element_type=F32).astype(BF16)
    scores = jnp.einsum('bskgh,btkh->bkgst', query, key_proj, preferred_element_type=F32) * (head_dim ** -0.5)
    causal = lax.broadcasted_iota(jnp.int32, (seq_len, seq_len), 0) >= lax.broadcasted_iota(jnp.int32, (seq_len, seq_len), 1)
    attn_probs = jax.nn.softmax(jnp.where(causal, scores, -1e30), axis=-1).astype(BF16)
    mixed = jnp.einsum('bkgst,btkh->bskgh', attn_probs, value, preferred_element_type=F32).astype(BF16)
    out_heads = w_out.reshape(kv_heads, group, head_dim, model_dim)
    projected = jnp.einsum('bskgh,kghd->bsd', mixed, out_heads, preferred_element_type=F32)
    return (hidden.astype(F32) + projected).astype(BF16)


def routing_rows(normed, w_router, routes, ep_size, local_count):
    halves, half_len, model_dim = normed.shape
    num_experts = w_router.shape[1]
    logits = jnp.einsum('htd,de->het', normed, w_router, preferred_element_type=F32)
    experts = lax.broadcasted_iota(jnp.int32, (1, num_experts, 1, 1), 1)
    chosen = jnp.any(jnp.swapaxes(routes, 1, 2)[:, None, :, :] == experts, axis=2)
    masked = jnp.where(chosen, logits, -jnp.inf)
    weights = jnp.exp(masked - jnp.max(masked, axis=1, keepdims=True))
    gates = weights / jnp.sum(weights, axis=1, keepdims=True)
    before = (lax.broadcasted_iota(jnp.int32, (half_len, half_len), 0) < lax.broadcasted_iota(jnp.int32, (half_len, half_len), 1)).astype(BF16)
    place = jnp.einsum('het,ts->hes', chosen.astype(BF16), before, preferred_element_type=F32)
    place = jnp.where(chosen, place, -1.0)
    gates = gates.reshape(halves, ep_size, local_count, half_len)
    place = place.reshape(halves, ep_size, local_count, half_len)
    pad = jnp.zeros((halves, ep_size, 8 - 2 * local_count, half_len), F32)
    return jnp.swapaxes(jnp.concatenate([gates, place, pad], axis=2), 0, 1)


def moe_kernel(
    ep_size, rows_half,
    u_ref, meta_ref, res_ref, wg_ref, wu_ref, wd_ref, sg_ref, su_ref, sd_ref, out_ref,
    ub, mb, wg, wu, wd, sg, su, sd, acc, xb, hb, yb, keep, dsend, drecv, isend, rbuf,
    wsem, shsem, lsem, fs, fr, uss, urs, mss, mrs, dss, drs, iss, irs, credit,
):
    chips = ep_size // 2
    me = lax.axis_index('ep')
    chip, core = me // 2, me % 2
    other = 1 - core
    sib = 2 * chip + other
    left = 2 * ((chip + chips - 1) % chips) + core
    right = 2 * ((chip + 1) % chips) + core
    ff = wg.shape[2]
    model_dim = wg.shape[1]
    half_len = ub.shape[2]
    n_ff, n_out = ff // CHUNK, model_dim // CHUNK

    def remote(src, dst, send, recv, device):
        return pltpu.make_async_remote_copy(src_ref=src, dst_ref=dst, send_sem=send, recv_sem=recv, device_id={'ep': device}, device_id_type=MESH)

    def shared_piece(j, slot):
        cols = pl.ds(pl.multiple_of(j * CHUNK, CHUNK), CHUNK)
        return (
            pltpu.make_async_copy(sg_ref.at[:, cols], sg.at[slot], shsem.at[slot, 0]),
            pltpu.make_async_copy(su_ref.at[:, cols], su.at[slot], shsem.at[slot, 1]),
            pltpu.make_async_copy(sd_ref.at[cols, :], sd.at[slot], shsem.at[slot, 2]),
        )

    def expert_weights(e):
        return (
            pltpu.make_async_copy(wg_ref.at[e], wg.at[e], wsem.at[e, 0]),
            pltpu.make_async_copy(wu_ref.at[e], wu.at[e], wsem.at[e, 1]),
            pltpu.make_async_copy(wd_ref.at[e], wd.at[e], wsem.at[e, 2]),
        )

    own_u = [pltpu.make_async_copy(u_ref.at[h], ub.at[slot, core], lsem.at[h]) for h, slot in ((0, OWN0), (1, OWN1))]
    own_m = [pltpu.make_async_copy(meta_ref.at[me, h], mb.at[slot, core], lsem.at[2 + h]) for h, slot in ((0, OWN0), (1, OWN1))]
    for copy in own_u:
        copy.start()
    for copy in own_m:
        copy.start()
    for copy in shared_piece(0, 0):
        copy.start()

    barrier = pltpu.get_barrier_semaphore()
    for step in range(1, ep_size):
        pl.semaphore_signal(barrier, inc=1, device_id={'ep': (me + step) % ep_size}, device_id_type=MESH)
    pl.semaphore_wait(barrier, ep_size - 1)

    def ring_u(src, slot, device):
        return remote(src, ub.at[slot, core], uss.at[slot], urs.at[slot], device)

    def partner_u(src, slot):
        return remote(src, ub.at[slot, core], fs.at[slot], fr.at[slot], sib)

    def partner_in(slot):
        return remote(ub.at[slot, other], ub.at[slot, other], fs.at[slot], fr.at[slot], sib)

    ring_u(u_ref.at[0], LEFT0, right).start()
    ring_u(u_ref.at[1], RIGHT1, left).start()
    partner_u(u_ref.at[0], OWN0).start()
    partner_u(u_ref.at[1], OWN1).start()

    meta_sends = []
    for hop, slots in ((0, (OWN0, OWN1)), (1, (LEFT0, LEFT1)), (2, (OPP0, OPP1)), (3, (RIGHT0, RIGHT1))):
        for flip in range(2):
            if hop == 0 and flip == 0:
                continue
            dest = 2 * ((chip + hop) % chips) + (core + flip) % 2
            for h, slot in enumerate(slots):
                meta_sends.append(remote(meta_ref.at[dest, h], mb.at[slot, core], mss.at[slot, flip], mrs.at[slot, core], dest))
    for copy in meta_sends:
        copy.start()

    for e in range(2):
        for copy in expert_weights(e):
            copy.start()
    for copy in own_u:
        copy.wait()
    for copy in own_m:
        copy.wait()

    for h in range(2):
        acc[h] = res_ref[h].astype(F32)

    def shared_step(j, carry):
        slot = j % 2

        @pl.when(j + 1 < n_ff)
        def _():
            for copy in shared_piece(j + 1, (j + 1) % 2):
                copy.start()

        for copy in shared_piece(j, slot):
            copy.wait()
        for h, own in ((0, OWN0), (1, OWN1)):
            rows = ub[own, core]
            gate_act = jnp.dot(rows, sg[slot], preferred_element_type=F32)
            up_act = jnp.dot(rows, su[slot], preferred_element_type=F32)
            act = (jax.nn.silu(gate_act) * up_act).astype(BF16)
            acc[h] += jnp.dot(act, sd[slot], preferred_element_type=F32)
        return carry

    lax.fori_loop(0, n_ff, shared_step, 0)

    def partial_copy(n):
        return remote(dsend.at[n % 2], drecv.at[n % 2], dss.at[n], drs.at[n], sib)

    def ring_copy(n):
        device = 2 * ((chip + 1 + (chips - 2) * (n % 2)) % chips) + core
        return remote(isend.at[n - 1], rbuf.at[n - 1], iss.at[n], irs.at[n], device)

    def merge(n):
        slot = n % 2
        partial_copy(n).wait_recv()

        @pl.when(jnp.logical_or(n == OWN0, n == OWN1))
        def _():
            acc[n // (UNITS - 1)] += keep[slot] + drecv[slot]

        @pl.when(jnp.logical_and(n != OWN0, n < LEFT0))
        def _():
            isend[n - 1] = keep[slot] + drecv[slot]

        for unit in (LEFT0, RIGHT1):
            @pl.when(n == unit)
            def _():
                ring_copy(unit - LEFT0 + OPP0).wait_recv()
                isend[unit - 1] = keep[slot] + drecv[slot] + rbuf[unit - LEFT0]

        @pl.when(n + 2 < UNITS)
        def _():
            pl.semaphore_signal(credit.at[slot], inc=1, device_id={'ep': sib}, device_id_type=MESH)

        @pl.when(jnp.logical_and(n != OWN0, n != OWN1))
        def _():
            ring_copy(n).start()

    def unit_step(n, carry):
        @pl.when(n == OPP0)
        def _():
            for slot in (OPP0, OPP1):
                ring_u(ub.at[slot, core], slot, left).wait_recv()
                partner_u(ub.at[slot, core], slot).start()

        partner_in(n).wait_recv()
        for part, kk in ((0, other), (1, core)):
            @pl.when(jnp.logical_or(jnp.logical_and(n != OWN0, n != OWN1), kk != core))
            def _():
                remote(mb.at[n, kk], mb.at[n, kk], mss.at[n, 0], mrs.at[n, kk], sib).wait_recv()

        for part, kk in ((0, other), (1, core)):
            rows = ub[n, kk]
            for e in range(2):
                place = mb[n, kk, 2 + e:3 + e, :].astype(jnp.int32)
                pick = (place == lax.broadcasted_iota(jnp.int32, (rows_half, half_len), 0)).astype(BF16)
                xb[e, part * rows_half:(part + 1) * rows_half, :] = jnp.dot(pick, rows, preferred_element_type=F32).astype(BF16)

        def expert_step(e, carry):
            @pl.when(n == OWN0)
            def _():
                for copy in expert_weights(e):
                    copy.wait()

            @pl.when(jnp.logical_and(n == OWN0, e == 1))
            def _():
                for slot, opp, device, own in ((LEFT0, OPP0, right, 1), (RIGHT1, OPP1, left, 0)):
                    ring_u(ub.at[slot, core], slot, device).wait_recv()
                    ring_u(ub.at[slot, core], opp, device).start()
                    ring_u(u_ref.at[own], LEFT1 if own == 1 else RIGHT0, device).start()
                    partner_u(ub.at[slot, core], slot).start()

            @pl.when(jnp.logical_and(n == OPP1, e == 1))
            def _():
                for slot, device in ((LEFT1, right), (RIGHT0, left)):
                    ring_u(ub.at[slot, core], slot, device).wait_recv()
                    partner_u(ub.at[slot, core], slot).start()

            rows = xb[e]

            def up_step(j, carry):
                cols = pl.ds(pl.multiple_of(j * CHUNK, CHUNK), CHUNK)
                gate_act = jnp.dot(rows, wg[e, :, cols], preferred_element_type=F32)
                up_act = jnp.dot(rows, wu[e, :, cols], preferred_element_type=F32)
                hb[:, cols] = (jax.nn.silu(gate_act) * up_act).astype(BF16)
                return carry

            lax.fori_loop(0, n_ff, up_step, 0)

            @pl.when(jnp.logical_and(n > 0, e == 0))
            def _():
                merge(n - 1)

            def down_step(j, carry):
                cols = pl.ds(pl.multiple_of(j * CHUNK, CHUNK), CHUNK)
                yb[e, :, cols] = jnp.dot(hb[...], wd[e, :, cols], preferred_element_type=F32).astype(BF16)
                return carry

            lax.fori_loop(0, n_out, down_step, 0)
            return carry

        lax.fori_loop(0, 2, expert_step, 0)

        @pl.when(n >= 2)
        def _():
            partial_copy(n - 2).wait_send()
            pl.semaphore_wait(credit.at[n % 2], 1)

        for part, kk in ((0, other), (1, core)):
            columns = jnp.transpose(mb[n, kk])
            picks = []
            for e in range(2):
                place = columns[:, 2 + e:3 + e].astype(jnp.int32)
                picks.append((place == lax.broadcasted_iota(jnp.int32, (half_len, rows_half), 1)).astype(BF16))
            target = dsend if part == 0 else keep

            for j in range(n_out):
                cols = pl.ds(j * CHUNK, CHUNK)
                total = None
                for e in range(2):
                    chosen = jnp.dot(picks[e], yb[e, part * rows_half:(part + 1) * rows_half, cols], preferred_element_type=F32)
                    term = columns[:, e:e + 1] * chosen
                    total = term if total is None else total + term
                target[n % 2, :, cols] = total
        partial_copy(n).start()
        return carry

    lax.fori_loop(0, UNITS, unit_step, 0)
    merge(UNITS - 1)

    for h, slots in ((0, (RIGHT0, LEFT0)), (1, (LEFT1, RIGHT1))):
        for slot in slots:
            ring_copy(slot).wait_recv()
        out_ref[h] = (acc[h] + rbuf[slots[0] - 1] + rbuf[slots[1] - 1]).astype(BF16)

    for slot in (OPP0, OPP1, LEFT1, RIGHT0, LEFT0, RIGHT1):
        ring_u(ub.at[slot, core], slot, right).wait_send()
        ring_copy(slot).wait_send()
    for slot in range(UNITS):
        partner_u(ub.at[slot, core], slot).wait_send()
    for copy in meta_sends:
        copy.wait_send()
    for n in (UNITS - 2, UNITS - 1):
        partial_copy(n).wait_send()


def moe_layer(u, meta, residual, w_gate, w_up, w_down, shared_gate, shared_up, shared_down, ep_size, rows_half, layer):
    halves, half_len, model_dim = u.shape
    ff = w_gate.shape[2]
    anyspec = pl.BlockSpec(memory_space=pl.ANY)
    vmem = pl.BlockSpec(memory_space=pltpu.VMEM)
    block = (half_len, model_dim)
    dma = pltpu.SemaphoreType.DMA
    return pl.pallas_call(
        functools.partial(moe_kernel, ep_size, rows_half),
        out_shape=jax.ShapeDtypeStruct(u.shape, BF16),
        in_specs=[anyspec, anyspec, vmem, anyspec, anyspec, anyspec, anyspec, anyspec, anyspec],
        out_specs=vmem,
        scratch_shapes=[
            pltpu.VMEM((UNITS, 2) + block, BF16),
            pltpu.VMEM((UNITS, 2, 8, half_len), F32),
            pltpu.VMEM((2, model_dim, ff), BF16),
            pltpu.VMEM((2, model_dim, ff), BF16),
            pltpu.VMEM((2, ff, model_dim), BF16),
            pltpu.VMEM((2, model_dim, CHUNK), BF16),
            pltpu.VMEM((2, model_dim, CHUNK), BF16),
            pltpu.VMEM((2, CHUNK, model_dim), BF16),
            pltpu.VMEM((2,) + block, F32),
            pltpu.VMEM((2, 2 * rows_half, model_dim), BF16),
            pltpu.VMEM((2 * rows_half, ff), BF16),
            pltpu.VMEM((2, 2 * rows_half, model_dim), BF16),
            pltpu.VMEM((2,) + block, F32),
            pltpu.VMEM((2,) + block, F32),
            pltpu.VMEM((2,) + block, F32),
            pltpu.VMEM((6,) + block, F32),
            pltpu.VMEM((6,) + block, F32),
            dma((2, 3)), dma((2, 3)), dma((4,)),
            dma((UNITS,)), dma((UNITS,)), dma((UNITS,)), dma((UNITS,)),
            dma((UNITS, 2)), dma((UNITS, 2)),
            dma((UNITS,)), dma((UNITS,)), dma((UNITS,)), dma((UNITS,)),
            pltpu.SemaphoreType.REGULAR((2,)),
        ],
        compiler_params=pltpu.CompilerParams(collective_id=layer, has_side_effects=True, vmem_limit_bytes=67043328),
        name='moe_layer',
    )(u, meta, residual, w_gate, w_up, w_down, shared_gate, shared_up, shared_down)


def layer_step(hidden, layer_params, ep_size, layer):
    (attn_gain, w_query, w_key, w_value, w_out, moe_gain, w_router, routes, w_gate, w_up, w_down, shared_gate, shared_up, shared_down) = layer_params
    batch, seq_len, model_dim = hidden.shape
    local_count = w_gate.shape[0]
    num_experts = local_count * ep_size
    rows_half = 3 * seq_len * routes.shape[-1] // num_experts
    residual = attention_block(hidden, attn_gain, w_query, w_key, w_value, w_out)
    normed = rms_norm(residual, moe_gain)
    meta = routing_rows(normed, w_router, routes, ep_size, local_count)
    return moe_layer(normed, meta, residual, w_gate, w_up, w_down, shared_gate, shared_up, shared_down, ep_size, rows_half, layer)


def solution(mesh):
    ep_size = mesh.shape['ep']
    token_spec = P(('dp', 'ep'))
    layer_specs = (P(), P(), P(), P(), P(), P(), P(), token_spec, P('ep'), P('ep'), P('ep'), P(), P(), P())
    in_specs = (token_spec,) + layer_specs + layer_specs

    def local_step(tokens, *params):
        hidden = tokens
        for layer in range(2):
            hidden = layer_step(hidden, params[14 * layer:14 * layer + 14], ep_size, layer)
        return hidden

    return jax.shard_map(local_step, mesh=mesh, in_specs=in_specs, out_specs=token_spec, check_vma=False)
```

time: 1070 us -> 376 us (0.35)
  Pallas kernels: 0 us -> 320 us
  local copies, waits for them, and re-layouts: 311 us -> 6.79 us
  waiting for transfers between devices: 249 us -> 0 us
  matrix products: 252 us -> 27.8 us
  blocking collectives: 142 us -> 0 us
  other arithmetic: 84.9 us -> 20.7 us
  starting transfers between devices: 20.6 us -> 0 us
    pallas_call x0 -> x2, Pallas kernels: none -> 320 us  [moe_layer(): pl.pallas_call(functools.partial(moe_kernel, ep_size, rows_half), out_sha...]
    gather x70 -> x0, local copies, waits for them, and re-layouts: 257 us -> none  [the longest x4 68.6 us: dispatch_plan(): slot_token = order[jnp.minimum(slot_src, num_rows - 1)] // top_k]
    all_to_all x3 -> x0, waiting for transfers between devices: 249 us -> none  [the longest x2 137 us: moe_layer(): returned = lax.all_to_all(expert_out, 'ep', 0, 0, tiled=True)]
    dot_general x18 -> x8, matrix products: 242 us -> 19.8 us  [the longest x2 6.93 us: attention_block(): jnp.einsum('bskgh,btkh->bkgst', query, key_proj, preferred_element_type=F32)]
    all_to_all x1 -> x0, blocking collectives: 142 us -> none  [moe_layer(): received = lax.all_to_all(send, 'ep', 0, 0, tiled=True)]
    convert_element_type x4 -> x0, local copies, waits for them, and re-layouts: 28.1 us -> none  [the longest x2 17.3 us: moe_layer(): routed = jnp.sum(gates[:, :, None] * picked.astype(jnp.float32), axis=1)]
    all_to_all x3 -> x0, starting transfers between devices: 20.6 us -> none  [the longest x2 12.9 us: moe_layer(): returned = lax.all_to_all(expert_out, 'ep', 0, 0, tiled=True)]
    select_n x58 -> x0, other arithmetic: 19.3 us -> none  [the longest x2 17.1 us: moe_layer(): jnp.where(slot_used[:, :, None], normed[slot_token], jnp.zeros((), jnp.bf...]
  transfers between devices with their start and end apart: 3 -> 0, of which waited for: 3 -> 0; matrix products, arithmetic and copies ran while one was open for 16% -> 0% of each run, Pallas kernels for 0% -> 0%
where the time goes in v1:
time: 376 us
  Pallas kernels  320 us (85%)
  matrix products  27.8 us (7%)
  other arithmetic  20.7 us (6%)
  local copies, waits for them, and re-layouts  6.79 us (2%)
    pallas_call x2, Pallas kernels, moe_layer(): pl.pallas_call(functools.partial(moe_kernel, ep_size, rows_half), out_sha...  320 us
    sub x2, other arithmetic, attention_block(): jax.nn.softmax(jnp.where(causal, scores, -1e+30), axis=-1).astype(BF16)  14.1 us

profile of v1, /device:TPU:81, one launch (start us, length us, event | category | flops | bytes accessed | tf_op | source)
XLA Modules:
  0.0 375.5 jit_solution(8330626611506006540)
XLA Ops:
  0.0 1.5 fusion.12
  1.5 0.7 convert_element_type.85
  2.2 3.3 fusion.48
  5.6 3.5 fusion.77
  9.1 0.0 copy-start.18
  9.1 7.1 %fusion.115 = (f32[2,2,4,256]{3,2,1,0:T(4,128)S(1)}, f32[2,2,4,256,256]{3,4,2,1,0:T(8,128)}) fusion(f32[2,2,256,256,4]{3,2,4,1,0:T(8,128)} %fusion.77, pred[256,256]{0,1:T(8,128)(4,1)S(1)} %iota_compare_fusion.1), kind=kOutput, calls=%fused_computation.115 | output fusion | flops 6291711 | bytes 8470528 | tf_op jit(solution)/shard_map/sub | solution.py:38
  16.2 3.5 fusion.61
  19.7 3.0 fusion.6
  22.8 0.9 copy-done.3
  23.7 0.3 fusion.8.u_ref
  24.1 0.9 copy-done
  25.0 0.4 fusion.116
  25.5 0.2 convolution_select_fusion.1
  25.7 0.1 pad.5.clone
  25.8 0.5 copy-done.14
  26.3 0.7 maximum_bitcast_fusion.meta_ref
  27.0 161.2 %moe_layer.2 = bf16[2,256,1024]{2,1,0:T(8,128)(2,1)} custom-call(bf16[2,256,1024]{2,1,0:T(8,128)(2,1)} %copy-done, f32[8,2,8,256]{3,2,1,0:T(8,128)} %maximum_bitcast_fusion.meta_ref, bf16[2,256,1024]{2,1,0:T(8,128)(2,1)} %copy-done.3, bf16[2,1024,1792]{2,1,0:T(8,128)(2,1)} %wg_ref.2, bf16[2,1024,1792]{2,1,0:T(8,128)(2,1)} %wu_ref.2, ...), custom_call_target="tpu_custom_call" | custom-call | tf_op jit(solution)/shard_map/moe_layer/pallas_call | solution.py:317
  188.2 1.5 fusion.16
  189.8 0.7 convert_element_type.98
  190.4 3.3 fusion.51
  193.8 3.5 fusion.76
  197.3 7.1 %fusion.117 = (f32[2,2,4,256]{3,2,1,0:T(4,128)S(1)}, f32[2,2,4,256,256]{3,4,2,1,0:T(8,128)}) fusion(f32[2,2,256,256,4]{3,2,4,1,0:T(8,128)} %fusion.76, pred[256,256]{0,1:T(8,128)(4,1)S(1)} %copy-done.9), kind=kOutput, calls=%fused_computation.117 | output fusion | flops 6291711 | bytes 8470528 | tf_op jit(solution)/shard_map/sub | solution.py:38
  204.4 3.5 fusion.58
  207.9 3.0 fusion.9
  211.0 0.9 copy-done.4
  211.9 0.3 fusion.11.u_ref
  212.3 0.9 copy-done.1
  213.2 0.4 fusion.118
  213.7 0.2 convolution_select_fusion
  213.9 0.7 maximum_bitcast_fusion.1.meta_ref
  214.6 158.6 %moe_layer.3 = bf16[2,256,1024]{2,1,0:T(8,128)(2,1)} custom-call(bf16[2,256,1024]{2,1,0:T(8,128)(2,1)} %copy-done.1, f32[8,2,8,256]{3,2,1,0:T(8,128)} %maximum_bitcast_fusion.1.meta_ref, bf16[2,256,1024]{2,1,0:T(8,128)(2,1)} %copy-done.4, bf16[2,1024,1792]{2,1,0:T(8,128)(2,1)} %wg_ref.3, bf16[2,1024,1792]{2,1,0:T(8,128)(2,1)} %wu_ref.3, ...), custom_call_target="tpu_custom_call" | custom-call | tf_op jit(solution)/shard_map/moe_layer/pallas_call | solution.py:317
  373.3 2.3 copy.155
  (54 shorter events, 0.4 us)
Async XLA Ops:
  2.2 3.3 copy-start.5
  2.2 3.3 copy-start.6
  9.1 7.1 %copy-start.8 = (pred[256,256]{0,1:T(8,128)(4,1)}, pred[256,256]{0,1:T(8,128)(4,1)S(1)}, u32[]{:S(2)}) copy-start(pred[256,256]{0,1:T(8,128)(4,1)S(1)} %iota_compare_fusion.1) | copy-start | bytes 196612
  9.1 7.1 %copy-start.18 = (bf16[1024,2,128]{2,1,0:T(2,128)(2,1)S(1)}, bf16[1024,2,128]{2,1,0:T(2,128)(2,1)}, u32[]{:S(2)}) copy-start(bf16[1024,2,128]{2,1,0:T(2,128)(2,1)} %param.33) | copy-start | bytes 1572868
  19.7 3.0 copy-start.16
  22.7 1.0 copy-start.3
  22.7 1.3 copy-start.12
  22.7 2.3 copy-start.10
  24.0 1.0 copy-start
  25.8 0.5 copy-start.14
  190.4 3.3 copy-start.2
  190.4 3.3 copy-start.7
  193.8 3.5 copy-start.9
  197.3 7.1 %copy-start.19 = (bf16[1024,2,128]{2,1,0:T(2,128)(2,1)S(1)}, bf16[1024,2,128]{2,1,0:T(2,128)(2,1)}, u32[]{:S(2)}) copy-start(bf16[1024,2,128]{2,1,0:T(2,128)(2,1)} %param.47) | copy-start | bytes 1572868
  207.9 3.1 copy-start.17
  210.9 1.0 copy-start.4
  210.9 1.3 copy-start.13
  210.9 2.3 copy-start.11
  210.9 3.0 copy-start.15
  212.2 1.0 copy-start.1

commit v2 on v1

v2 whole, which is shorter than its diff:
```python
import functools

import jax
import jax.numpy as jnp
from jax import lax
from jax.experimental import pallas as pl
from jax.experimental.pallas import tpu as pltpu
from jax.sharding import PartitionSpec as P

NORM_EPS = 1e-6
MESH = pl.DeviceIdType.MESH
F32 = jnp.float32
BF16 = jnp.bfloat16

OWN0, OPP0, OPP1, RIGHT0, LEFT0, RIGHT1, LEFT1, OWN1 = range(8)
UNITS = 8
CHUNK = 256
LAYERS = 2


def rms_norm(hidden, gain):
    inv_rms = lax.rsqrt(jnp.mean(hidden * hidden, axis=-1, keepdims=True) + NORM_EPS)
    return (hidden * inv_rms * gain).astype(BF16)


def body(
    ep_size, heads, kv_heads, top_k, rows_half,
    x_ref, *refs,
):
    layer_refs = (refs[:12], refs[12:24])
    (
        out_ref,
        wqkv, wo, ub, mb, ms, wg, wu, wd, sg, su, sd, acc, xb, hb, keep, dsend, drecv, isend, rbuf,
        asem, wsem, shsem, fs, fr, uss, urs, mss, mrs, dss, drs, iss, irs, credit,
    ) = refs[24:]
    chips = ep_size // 2
    me = lax.axis_index('ep')
    chip, core = me // 2, me % 2
    other = 1 - core
    sib = 2 * chip + other
    left = 2 * ((chip + chips - 1) % chips) + core
    right = 2 * ((chip + 1) % chips) + core
    ff = wg.shape[2]
    model_dim = wg.shape[1]
    half_len = ub.shape[2]
    head_dim = model_dim // heads
    group = heads // kv_heads
    n_ff, n_out = ff // CHUNK, model_dim // CHUNK

    def remote(src, dst, send, recv, device):
        return pltpu.make_async_remote_copy(src_ref=src, dst_ref=dst, send_sem=send, recv_sem=recv, device_id={'ep': device}, device_id_type=MESH)

    def attention_weights(layer):
        wqkv_ref, wo_ref = layer_refs[layer][1:3]
        return (
            pltpu.make_async_copy(wqkv_ref, wqkv, asem.at[0]),
            pltpu.make_async_copy(wo_ref, wo, asem.at[1]),
        )

    def shared_piece(layer, j, slot):
        sg_ref, su_ref, sd_ref = layer_refs[layer][9:12]
        cols = pl.ds(pl.multiple_of(j * CHUNK, CHUNK), CHUNK)
        return (
            pltpu.make_async_copy(sg_ref.at[:, cols], sg.at[slot], shsem.at[slot, 0]),
            pltpu.make_async_copy(su_ref.at[:, cols], su.at[slot], shsem.at[slot, 1]),
            pltpu.make_async_copy(sd_ref.at[cols, :], sd.at[slot], shsem.at[slot, 2]),
        )

    def expert_weights(layer, e):
        wg_ref, wu_ref, wd_ref = layer_refs[layer][6:9]
        return (
            pltpu.make_async_copy(wg_ref.at[e], wg.at[e], wsem.at[e, 0]),
            pltpu.make_async_copy(wu_ref.at[e], wu.at[e], wsem.at[e, 1]),
            pltpu.make_async_copy(wd_ref.at[e], wd.at[e], wsem.at[e, 2]),
        )

    def start_for(layer, make):
        for which in range(LAYERS):
            @pl.when(layer == which)
            def _():
                for copy in make(which):
                    copy.start()

    x_copy = pltpu.make_async_copy(x_ref, out_ref, asem.at[2])
    x_copy.start()
    for copy in attention_weights(0):
        copy.start()

    barrier = pltpu.get_barrier_semaphore()
    for step in range(1, ep_size):
        pl.semaphore_signal(barrier, inc=1, device_id={'ep': (me + step) % ep_size}, device_id_type=MESH)
    x_copy.wait()
    pl.semaphore_wait(barrier, ep_size - 1)

    def ring_u(src, slot, device):
        return remote(src, ub.at[slot, core], uss.at[slot], urs.at[slot], device)

    def arrived(slot):
        ring_u(ub.at[slot, core], slot, left).wait_recv()

    def partner_u(slot):
        return remote(ub.at[slot, core], ub.at[slot, core], fs.at[slot], fr.at[slot], sib)

    def partner_in(slot):
        return remote(ub.at[slot, other], ub.at[slot, other], fs.at[slot], fr.at[slot], sib)

    hops = ((0, (OWN0, OWN1)), (1, (LEFT0, LEFT1)), (2, (OPP0, OPP1)), (3, (RIGHT0, RIGHT1)))

    def meta_sends(h):
        copies = []
        for hop, slots in hops:
            for flip in range(2):
                if hop == 0 and flip == 0:
                    continue
                dest = 2 * ((chip + hop) % chips) + (core + flip) % 2
                slot = slots[h]
                copies.append(remote(ms.at[h, dest], mb.at[slot, core], mss.at[slot, flip], mrs.at[slot, core], dest))
        return copies

    def partial_copy(slot):
        return remote(dsend.at[slot], drecv.at[slot], dss.at[slot], drs.at[slot], sib)

    def ring_copy(n):
        device = 2 * ((chip + 1 + (chips - 2) * ((n + 1) % 2)) % chips) + core
        return remote(isend.at[(n - 1) % 4], rbuf.at[n - 1], iss.at[n], irs.at[n], device)

    def finish(h):
        for n in (RIGHT0 + 2 * h, LEFT0 + 2 * h):
            ring_copy(n).wait_recv()
        out_ref[h] = (acc[h] + rbuf[RIGHT0 - 1 + 2 * h] + rbuf[LEFT0 - 1 + 2 * h]).astype(BF16)

    def per_layer(layer, index):
        return jnp.where(layer == 0, layer_refs[0][index][...].astype(F32), layer_refs[1][index][...].astype(F32))

    def attention_half(layer, h):
        normed = rms_norm(out_ref[h].astype(F32), per_layer(layer, 0))
        for j in range(wqkv.shape[1] // CHUNK):
            cols = slice(j * CHUNK, (j + 1) * CHUNK)
            hb[0:half_len, cols] = jnp.dot(normed, wqkv[:, cols], preferred_element_type=F32).astype(BF16)
        causal = lax.broadcasted_iota(jnp.int32, (half_len, half_len), 0) >= lax.broadcasted_iota(jnp.int32, (half_len, half_len), 1)
        for head in range(heads):
            kv = head // group
            query = hb[0:half_len, head * head_dim:(head + 1) * head_dim]
            keys = hb[0:half_len, (heads + kv) * head_dim:(heads + kv + 1) * head_dim]
            values = hb[0:half_len, (heads + kv_heads + kv) * head_dim:(heads + kv_heads + kv + 1) * head_dim]
            scores = lax.dot_general(query, keys, (((1,), (1,)), ((), ())), preferred_element_type=F32) * (head_dim ** -0.5)
            scores = jnp.where(causal, scores, -1e30)
            weights = jnp.exp(scores - jnp.max(scores, axis=-1, keepdims=True))
            probs = (weights / jnp.sum(weights, axis=-1, keepdims=True)).astype(BF16)
            xb[0, 0:half_len, head * head_dim:(head + 1) * head_dim] = jnp.dot(probs, values, preferred_element_type=F32).astype(BF16)
        for j in range(n_out):
            cols = slice(j * CHUNK, (j + 1) * CHUNK)
            projected = jnp.dot(xb[0, 0:half_len, :], wo[:, cols], preferred_element_type=F32)
            acc[h, :, cols] = (out_ref[h, :, cols].astype(F32) + projected).astype(BF16).astype(F32)
        ub[OWN1 * h, core] = rms_norm(acc[h], per_layer(layer, 3))

    def routing_half(layer, h):
        rows = ub[OWN1 * h, core]
        router = per_layer(layer, 4).astype(BF16)
        num_experts = router.shape[0]
        logits = lax.dot_general(router, rows, (((1,), (1,)), ((), ())), preferred_element_type=F32)
        picked = jnp.where(layer == 0, layer_refs[0][5][h], layer_refs[1][5][h])
        experts = lax.broadcasted_iota(jnp.int32, (num_experts, half_len), 0)
        chosen = picked[0:1, :] == experts
        for j in range(1, top_k):
            chosen = jnp.logical_or(chosen, picked[j:j + 1, :] == experts)
        masked = jnp.where(chosen, logits, -jnp.inf)
        weights = jnp.exp(masked - jnp.max(masked, axis=0, keepdims=True))
        gates = weights / jnp.sum(weights, axis=0, keepdims=True)
        before = (lax.broadcasted_iota(jnp.int32, (half_len, half_len), 0) < lax.broadcasted_iota(jnp.int32, (half_len, half_len), 1)).astype(BF16)
        place = jnp.dot(chosen.astype(F32).astype(BF16), before, preferred_element_type=F32)
        place = jnp.where(chosen, place, -1.0)
        for dest in range(ep_size):
            ms[h, dest, 0:2, :] = gates[2 * dest:2 * dest + 2, :]
            ms[h, dest, 2:4, :] = place[2 * dest:2 * dest + 2, :]
            ms[h, dest, 4:8, :] = jnp.zeros((4, half_len), F32)
        mb[OWN1 * h, core] = ms[h, me]

    def shared_expert(layer):
        def shared_step(j, carry):
            slot = j % 2

            @pl.when(j + 1 < n_ff)
            def _():
                start_for(layer, lambda which: shared_piece(which, j + 1, (j + 1) % 2))

            @pl.when(j == n_ff // 2)
            def _():
                arrived(RIGHT1)
                ring_u(ub.at[RIGHT1, core], OPP1, left).start()
                ring_u(ub.at[OWN0, core], RIGHT0, left).start()
                partner_u(RIGHT1).start()

            for copy in shared_piece(0, j, slot):
                copy.wait()
            for h, own in ((0, OWN0), (1, OWN1)):
                rows = ub[own, core]
                gate_act = jnp.dot(rows, sg[slot], preferred_element_type=F32)
                up_act = jnp.dot(rows, su[slot], preferred_element_type=F32)
                act = (jax.nn.silu(gate_act) * up_act).astype(BF16)
                acc[h] += jnp.dot(act, sd[slot], preferred_element_type=F32)
            return carry

        lax.fori_loop(0, n_ff, shared_step, 0)

    def merge(layer, n):
        slot = n % 2
        partial_copy(slot).wait_recv()

        @pl.when(jnp.logical_or(n == OWN0, n == OWN1))
        def _():
            acc[n // OWN1] += keep[slot] + drecv[slot]

        @pl.when(jnp.logical_and(n > 4, n < OWN1))
        def _():
            ring_copy(n - 4).wait_send()

        for low, high, add in ((OPP0, OPP1, None), (RIGHT0, RIGHT0, OPP0), (LEFT0, RIGHT1, None), (LEFT1, LEFT1, OPP1)):
            @pl.when(jnp.logical_and(n >= low, n <= high))
            def _():
                total = keep[slot] + drecv[slot]
                if add is not None:
                    ring_copy(add).wait_recv()
                    total = total + rbuf[add - 1]
                isend[(n - 1) % 4] = total

        @pl.when(UNITS * layer + n + 2 < UNITS * LAYERS)
        def _():
            pl.semaphore_signal(credit.at[slot], inc=1, device_id={'ep': sib}, device_id_type=MESH)

        @pl.when(jnp.logical_and(n != OWN0, n != OWN1))
        def _():
            ring_copy(n).start()

    def unit_step(layer, n):
        @pl.when(n == OPP0)
        def _():
            shared_expert(layer)
            arrived(OPP0)
            partner_u(OPP0).start()

        partner_in(n).wait_recv()
        for part, kk in ((0, other), (1, core)):
            @pl.when(jnp.logical_or(jnp.logical_and(n != OWN0, n != OWN1), kk != core))
            def _():
                remote(mb.at[n, kk], mb.at[n, kk], mss.at[n, 0], mrs.at[n, kk], sib).wait_recv()

        for part, kk in ((0, other), (1, core)):
            rows = ub[n, kk]
            for e in range(2):
                place = mb[n, kk, 2 + e:3 + e, :].astype(jnp.int32)
                pick = (place == lax.broadcasted_iota(jnp.int32, (rows_half, half_len), 0)).astype(BF16)
                xb[e, part * rows_half:(part + 1) * rows_half, :] = jnp.dot(pick, rows, preferred_element_type=F32).astype(BF16)

        def expert_step(e, carry):
            @pl.when(n == OWN0)
            def _():
                for copy in expert_weights(0, e):
                    copy.wait()

            @pl.when(jnp.logical_and(n == OPP0, e == 1))
            def _():
                arrived(OPP1)
                partner_u(OPP1).start()

            @pl.when(jnp.logical_and(n == OPP1, e == 1))
            def _():
                for slot in (LEFT1, RIGHT0):
                    arrived(slot)
                    partner_u(slot).start()

            rows = xb[e]
            for j in range(n_ff):
                cols = slice(j * CHUNK, (j + 1) * CHUNK)
                gate_act = jnp.dot(rows, wg[e, :, cols], preferred_element_type=F32)
                up_act = jnp.dot(rows, wu[e, :, cols], preferred_element_type=F32)
                hb[:, cols] = (jax.nn.silu(gate_act) * up_act).astype(BF16)

            @pl.when(jnp.logical_and(n == OWN0, e == 1))
            def _():
                arrived(LEFT0)
                ring_u(ub.at[LEFT0, core], OPP0, right).start()
                ring_u(ub.at[OWN1, core], LEFT1, right).start()
                partner_u(LEFT0).start()

            @pl.when(jnp.logical_and(n == LEFT0, e == 0))
            def _():
                for slot in range(UNITS):
                    partner_u(slot).wait_send()
                for slot in range(OPP0, OWN1):
                    ring_u(ub.at[slot, core], slot, right).wait_send()
                for h in range(2):
                    for copy in meta_sends(h):
                        copy.wait_send()

            @pl.when(jnp.logical_and(n > 0, e == 0))
            def _():
                merge(layer, n - 1)

            for j in range(n_out):
                cols = slice(j * CHUNK, (j + 1) * CHUNK)
                xb[e, :, cols] = jnp.dot(hb[...], wd[e, :, cols], preferred_element_type=F32).astype(BF16)
            return carry

        lax.fori_loop(0, 2, expert_step, 0)

        slot = n % 2

        @pl.when(UNITS * layer + n >= 2)
        def _():
            partial_copy(slot).wait_send()
            pl.semaphore_wait(credit.at[slot], 1)

        for part, kk in ((0, other), (1, core)):
            columns = jnp.transpose(mb[n, kk])
            picks = []
            for e in range(2):
                place = columns[:, 2 + e:3 + e].astype(jnp.int32)
                picks.append((place == lax.broadcasted_iota(jnp.int32, (half_len, rows_half), 1)).astype(BF16))
            target = dsend if part == 0 else keep
            for j in range(n_out):
                cols = slice(j * CHUNK, (j + 1) * CHUNK)
                total = None
                for e in range(2):
                    row = jnp.dot(picks[e], xb[e, part * rows_half:(part + 1) * rows_half, cols], preferred_element_type=F32)
                    term = columns[:, e:e + 1] * row
                    total = term if total is None else total + term
                target[slot, :, cols] = total
        partial_copy(slot).start()

    def layer_step(layer, carry):
        start_for(layer, lambda which: shared_piece(which, 0, 0))
        for e in range(2):
            start_for(layer, lambda which: expert_weights(which, e))

        def half_step(h, carry):
            @pl.when(layer > 0)
            def _():
                finish(h)

            @pl.when(h == 0)
            def _():
                for copy in attention_weights(0):
                    copy.wait()

            attention_half(layer, h)
            routing_half(layer, h)

            @pl.when(h == 0)
            def _():
                ring_u(ub.at[OWN0, core], LEFT0, right).start()
                partner_u(OWN0).start()
                for copy in meta_sends(0):
                    copy.start()

            @pl.when(h == 1)
            def _():
                ring_u(ub.at[OWN1, core], RIGHT1, left).start()
                partner_u(OWN1).start()
                for copy in meta_sends(1):
                    copy.start()
            return carry

        lax.fori_loop(0, 2, half_step, 0)

        @pl.when(layer + 1 < LAYERS)
        def _():
            for copy in attention_weights(1):
                copy.start()

        @pl.when(layer > 0)
        def _():
            for n in (RIGHT0, LEFT0, RIGHT1, LEFT1):
                ring_copy(n).wait_send()

        def step(n, carry):
            unit_step(layer, n)
            return carry

        lax.fori_loop(0, UNITS, step, 0)
        merge(layer, OWN1)
        return carry

    lax.fori_loop(0, LAYERS, layer_step, 0)
    for h in range(2):
        finish(h)
    for n in (RIGHT0, LEFT0, RIGHT1, LEFT1):
        ring_copy(n).wait_send()
    for slot in range(2):
        partial_copy(slot).wait_send()


def two_layers(tokens, layers, ep_size):
    halves, half_len, model_dim = tokens.shape
    operands = [tokens]
    anyspec = pl.BlockSpec(memory_space=pl.ANY)
    vmem = pl.BlockSpec(memory_space=pltpu.VMEM)
    specs = [anyspec]
    for params in layers:
        (attn_gain, w_query, w_key, w_value, w_out, moe_gain, w_router, routes, w_gate, w_up, w_down, shared_gate, shared_up, shared_down) = params
        heads, kv_heads = w_query.shape[1], w_key.shape[1]
        w_qkv = jnp.concatenate([w.reshape(model_dim, -1) for w in (w_query, w_key, w_value)], axis=1)
        operands += [
            attn_gain.reshape(1, model_dim), w_qkv, w_out.reshape(-1, model_dim), moe_gain.reshape(1, model_dim), w_router.T, jnp.swapaxes(routes, 1, 2),
            w_gate, w_up, w_down, shared_gate, shared_up, shared_down,
        ]
        specs += [vmem, anyspec, anyspec, vmem, vmem, vmem] + [anyspec] * 6
    ff = w_gate.shape[2]
    top_k = routes.shape[-1]
    num_experts = w_gate.shape[0] * ep_size
    rows_half = 3 * half_len * top_k // num_experts
    block = (half_len, model_dim)
    dma = pltpu.SemaphoreType.DMA
    return pl.pallas_call(
        functools.partial(body, ep_size, heads, kv_heads, top_k, rows_half),
        out_shape=jax.ShapeDtypeStruct(tokens.shape, BF16),
        in_specs=specs,
        out_specs=vmem,
        scratch_shapes=[
            pltpu.VMEM(w_qkv.shape, BF16),
            pltpu.VMEM((heads * w_query.shape[2], model_dim), BF16),
            pltpu.VMEM((UNITS, 2) + block, BF16),
            pltpu.VMEM((UNITS, 2, 8, half_len), F32),
            pltpu.VMEM((2, ep_size, 8, half_len), F32),
            pltpu.VMEM((2, model_dim, ff), BF16),
            pltpu.VMEM((2, model_dim, ff), BF16),
            pltpu.VMEM((2, ff, model_dim), BF16),
            pltpu.VMEM((2, model_dim, CHUNK), BF16),
            pltpu.VMEM((2, model_dim, CHUNK), BF16),
            pltpu.VMEM((2, CHUNK, model_dim), BF16),
            pltpu.VMEM((2,) + block, F32),
            pltpu.VMEM((2, 2 * rows_half, model_dim), BF16),
            pltpu.VMEM((2 * rows_half, ff), BF16),
            pltpu.VMEM((2,) + block, F32),
            pltpu.VMEM((2,) + block, F32),
            pltpu.VMEM((2,) + block, F32),
            pltpu.VMEM((4,) + block, F32),
            pltpu.VMEM((6,) + block, F32),
            dma((3,)), dma((2, 3)), dma((2, 3)),
            dma((UNITS,)), dma((UNITS,)), dma((UNITS,)), dma((UNITS,)),
            dma((UNITS, 2)), dma((UNITS, 2)),
            dma((2,)), dma((2,)), dma((UNITS,)), dma((UNITS,)),
            pltpu.SemaphoreType.REGULAR((2,)),
        ],
        compiler_params=pltpu.CompilerParams(collective_id=0, has_side_effects=True, vmem_limit_bytes=67043328),
        name='two_layers',
    )(*operands)


def solution(mesh):
    ep_size = mesh.shape['ep']
    token_spec = P(('dp', 'ep'))
    layer_specs = (P(), P(), P(), P(), P(), P(), P(), token_spec, P('ep'), P('ep'), P('ep'), P(), P(), P())
    in_specs = (token_spec,) + layer_specs + layer_specs

    def local_step(tokens, *params):
        return two_layers(tokens, (params[:14], params[14:]), ep_size)

    return jax.shard_map(local_step, mesh=mesh, in_specs=in_specs, out_specs=token_spec, check_vma=False)
```

time: 376 us -> 277 us (0.74)
  Pallas kernels: 320 us -> 263 us
  matrix products: 27.8 us -> 0 us
  other arithmetic: 20.7 us -> 3.6 us
    pallas_call x2 -> x1, Pallas kernels: 320 us -> 263 us  [two_layers(): pl.pallas_call(functools.partial(body, ep_size, heads, kv_heads, top_k, r...]
    dot_general x10 -> x0, matrix products: 26.9 us -> none  [the longest x2 7.08 us: attention_block(): jnp.einsum('bkgst,btkh->bskgh', attn_probs, value, preferred_element_type...]
    sub x2 -> x0, other arithmetic: 14.1 us -> none  [attention_block(): jax.nn.softmax(jnp.where(causal, scores, -1e+30), axis=-1).astype(BF16)]
    reshape x4 -> x6, local copies, waits for them, and re-layouts: 0.07 us -> 3.89 us  [the longest x2 1.53 us: two_layers(): w.reshape(model_dim, -1)]
where the time goes in v2:
time: 277 us
  Pallas kernels  263 us (95%)
  local copies, waits for them, and re-layouts  10.1 us (4%)
  other arithmetic  3.6 us (1%)
    pallas_call x1, Pallas kernels, two_layers(): pl.pallas_call(functools.partial(body, ep_size, heads, kv_heads, top_k, r...  263 us
    unnamed x17, local copies, waits for them, and re-layouts  6.17 us

profile of v2, /device:TPU:81, one launch (start us, length us, event | category | flops | bytes accessed | tf_op | source)
XLA Modules:
  0.0 276.6 jit_solution(6714505570941752504)
XLA Ops:
  0.0 1.4 copy_bitcast_fusion.2
  1.4 2.2 copy.42
  3.6 0.0 copy-start.1
  3.6 0.0 copy-start.2
  3.6 0.0 copy-start
  3.6 1.8 pad_maximum_fusion.1.refs_13_
  5.4 0.0 copy-done.1
  5.4 0.0 copy-done.2
  5.4 0.2 copy_bitcast_fusion.4
  5.6 1.0 copy-done
  6.7 0.6 copy.43
  7.3 0.0 copy-start.3
  7.3 0.0 copy-start.4
  7.3 0.0 copy-start.5
  7.3 0.0 copy-start.6
  7.3 1.8 pad_maximum_fusion.refs_1_
  9.1 0.0 copy-done.3
  9.1 0.6 reshape.36.refs_0_
  9.7 0.0 copy-done.4
  9.7 0.6 reshape.41.refs_3_
  10.3 0.0 copy-done.5
  10.3 0.6 reshape.42.refs_12_
  10.9 0.0 copy-done.6
  10.9 0.6 reshape.47.refs_15_
  11.5 262.9 %two_layers.1 = bf16[2,256,1024]{2,1,0:T(8,128)(2,1)} custom-call(bf16[2,256,1024]{2,1,0:T(8,128)(2,1)} %x_ref.1, bf16[1,1024]{1,0:T(2,128)(2,1)} %reshape.36.refs_0_, bf16[1024,1536]{1,0:T(8,128)(2,1)} %pad_maximum_fusion.refs_1_, bf16[1024,1024]{1,0:T(8,128)(2,1)} %bitcast.30, bf16[1,1024]{1,0:T(2,128)(2,1)} %reshape.41.refs_3_, ...), custom_call_target="tpu_custom_call" | custom-call | tf_op jit(solution)/shard_map/two_layers/pallas_call | solution.py:414
  274.4 2.3 copy.45
Async XLA Ops:
  3.6 1.9 copy-start.1
  3.6 1.9 copy-start.2
  3.6 3.0 %copy-start = (bf16[1024,8,128]{2,1,0:T(8,128)(2,1)S(1)}, bf16[1024,8,128]{2,1,0:T(8,128)(2,1)}, u32[]{:S(2)}) copy-start(bf16[1024,8,128]{2,1,0:T(8,128)(2,1)} %param.31) | copy-start | bytes 6291460
  7.3 1.8 copy-start.3
  7.3 2.4 copy-start.4
  7.3 3.0 %copy-start.5 = (bf16[1024]{0:T(1024)(128)(2,1)S(1)}, bf16[1024]{0:T(1024)(128)(2,1)}, u32[]{:S(2)}) copy-start(bf16[1024]{0:T(1024)(128)(2,1)} %param.44) | copy-start | bytes 6148
  7.3 3.6 %copy-start.6 = (bf16[1024]{0:T(1024)(128)(2,1)S(1)}, bf16[1024]{0:T(1024)(128)(2,1)}, u32[]{:S(2)}) copy-start(bf16[1024]{0:T(1024)(128)(2,1)} %param.49) | copy-start | bytes 6148

commit v3 on v2

--- a/solution.py
+++ b/solution.py
@@ -12,7 +12,7 @@
 F32 = jnp.float32
 BF16 = jnp.bfloat16
 
-OWN0, OPP0, OPP1, RIGHT0, LEFT0, RIGHT1, LEFT1, OWN1 = range(8)
+OWN0, LEFT0, OPP0, OPP1, RIGHT0, LEFT1, RIGHT1, OWN1 = range(8)
 UNITS = 8
 CHUNK = 256
 LAYERS = 2
@@ -27,12 +27,12 @@
     ep_size, heads, kv_heads, top_k, rows_half,
     x_ref, *refs,
 ):
-    layer_refs = (refs[:12], refs[12:24])
+    layer_refs = (refs[:14], refs[14:28])
     (
         out_ref,
         wqkv, wo, ub, mb, ms, wg, wu, wd, sg, su, sd, acc, xb, hb, keep, dsend, drecv, isend, rbuf,
         asem, wsem, shsem, fs, fr, uss, urs, mss, mrs, dss, drs, iss, irs, credit,
-    ) = refs[24:]
+    ) = refs[28:]
     chips = ep_size // 2
     me = lax.axis_index('ep')
     chip, core = me // 2, me % 2
@@ -51,14 +51,15 @@
         return pltpu.make_async_remote_copy(src_ref=src, dst_ref=dst, send_sem=send, recv_sem=recv, device_id={'ep': device}, device_id_type=MESH)
 
     def attention_weights(layer):
-        wqkv_ref, wo_ref = layer_refs[layer][1:3]
-        return (
-            pltpu.make_async_copy(wqkv_ref, wqkv, asem.at[0]),
-            pltpu.make_async_copy(wo_ref, wo, asem.at[1]),
-        )
+        copies, start = [], 0
+        for i, ref in enumerate(layer_refs[layer][1:4]):
+            copies.append(pltpu.make_async_copy(ref, wqkv.at[:, pl.ds(start, ref.shape[1])], asem.at[i]))
+            start += ref.shape[1]
+        copies.append(pltpu.make_async_copy(layer_refs[layer][4], wo, asem.at[3]))
+        return copies
 
     def shared_piece(layer, j, slot):
-        sg_ref, su_ref, sd_ref = layer_refs[layer][9:12]
+        sg_ref, su_ref, sd_ref = layer_refs[layer][11:14]
         cols = pl.ds(pl.multiple_of(j * CHUNK, CHUNK), CHUNK)
         return (
             pltpu.make_async_copy(sg_ref.at[:, cols], sg.at[slot], shsem.at[slot, 0]),
@@ -67,7 +68,7 @@
         )
 
     def expert_weights(layer, e):
-        wg_ref, wu_ref, wd_ref = layer_refs[layer][6:9]
+        wg_ref, wu_ref, wd_ref = layer_refs[layer][8:11]
         return (
             pltpu.make_async_copy(wg_ref.at[e], wg.at[e], wsem.at[e, 0]),
             pltpu.make_async_copy(wu_ref.at[e], wu.at[e], wsem.at[e, 1]),
@@ -81,7 +82,7 @@
                 for copy in make(which):
                     copy.start()
 
-    x_copy = pltpu.make_async_copy(x_ref, out_ref, asem.at[2])
+    x_copy = pltpu.make_async_copy(x_ref, out_ref, asem.at[4])
     x_copy.start()
     for copy in attention_weights(0):
         copy.start()
@@ -120,20 +121,31 @@
     def partial_copy(slot):
         return remote(dsend.at[slot], drecv.at[slot], dss.at[slot], drs.at[slot], sib)
 
+    def place_of(n):
+        return n - 1 - 3 * (n // LEFT1)
+
     def ring_copy(n):
-        device = 2 * ((chip + 1 + (chips - 2) * ((n + 1) % 2)) % chips) + core
-        return remote(isend.at[(n - 1) % 4], rbuf.at[n - 1], iss.at[n], irs.at[n], device)
+        device = right if n in (RIGHT0, RIGHT1) else left
+        return remote(isend.at[place_of(n)], rbuf.at[n - 1], iss.at[n, 0], irs.at[n, 0], device)
+
+    def opposite_copy(n, part):
+        rows = pl.ds(part * (half_len // 2), half_len // 2)
+        return remote(isend.at[place_of(n), rows], rbuf.at[n - 1, rows], iss.at[n, part], irs.at[n, part], (right, left)[part])
 
     def finish(h):
-        for n in (RIGHT0 + 2 * h, LEFT0 + 2 * h):
-            ring_copy(n).wait_recv()
-        out_ref[h] = (acc[h] + rbuf[RIGHT0 - 1 + 2 * h] + rbuf[LEFT0 - 1 + 2 * h]).astype(BF16)
+        from_left, from_right = RIGHT0 + (RIGHT1 - RIGHT0) * h, LEFT0 + (LEFT1 - LEFT0) * h
+        for n in (from_left, from_right):
+            remote(rbuf.at[n - 1], rbuf.at[n - 1], iss.at[n, 0], irs.at[n, 0], sib).wait_recv()
+        out_ref[h] = (acc[h] + rbuf[from_left - 1] + rbuf[from_right - 1]).astype(BF16)
 
     def per_layer(layer, index):
         return jnp.where(layer == 0, layer_refs[0][index][...].astype(F32), layer_refs[1][index][...].astype(F32))
 
+    def gain_of(layer, index):
+        return per_layer(layer, index).reshape(1, model_dim)
+
     def attention_half(layer, h):
-        normed = rms_norm(out_ref[h].astype(F32), per_layer(layer, 0))
+        normed = rms_norm(out_ref[h].astype(F32), gain_of(layer, 0))
         for j in range(wqkv.shape[1] // CHUNK):
             cols = slice(j * CHUNK, (j + 1) * CHUNK)
             hb[0:half_len, cols] = jnp.dot(normed, wqkv[:, cols], preferred_element_type=F32).astype(BF16)
@@ -152,14 +164,14 @@
             cols = slice(j * CHUNK, (j + 1) * CHUNK)
             projected = jnp.dot(xb[0, 0:half_len, :], wo[:, cols], preferred_element_type=F32)
             acc[h, :, cols] = (out_ref[h, :, cols].astype(F32) + projected).astype(BF16).astype(F32)
-        ub[OWN1 * h, core] = rms_norm(acc[h], per_layer(layer, 3))
+        ub[OWN1 * h, core] = rms_norm(acc[h], gain_of(layer, 5))
 
     def routing_half(layer, h):
         rows = ub[OWN1 * h, core]
-        router = per_layer(layer, 4).astype(BF16)
+        router = per_layer(layer, 6).astype(BF16)
         num_experts = router.shape[0]
         logits = lax.dot_general(router, rows, (((1,), (1,)), ((), ())), preferred_element_type=F32)
-        picked = jnp.where(layer == 0, layer_refs[0][5][h], layer_refs[1][5][h])
+        picked = jnp.where(layer == 0, layer_refs[0][7][h], layer_refs[1][7][h])
         experts = lax.broadcasted_iota(jnp.int32, (num_experts, half_len), 0)
         chosen = picked[0:1, :] == experts
         for j in range(1, top_k):
@@ -184,13 +196,6 @@
             def _():
                 start_for(layer, lambda which: shared_piece(which, j + 1, (j + 1) % 2))
 
-            @pl.when(j == n_ff // 2)
-            def _():
-                arrived(RIGHT1)
-                ring_u(ub.at[RIGHT1, core], OPP1, left).start()
-                ring_u(ub.at[OWN0, core], RIGHT0, left).start()
-                partner_u(RIGHT1).start()
-
             for copy in shared_piece(0, j, slot):
                 copy.wait()
             for h, own in ((0, OWN0), (1, OWN1)):
@@ -211,31 +216,47 @@
         def _():
             acc[n // OWN1] += keep[slot] + drecv[slot]
 
-        @pl.when(jnp.logical_and(n > 4, n < OWN1))
-        def _():
-            ring_copy(n - 4).wait_send()
-
-        for low, high, add in ((OPP0, OPP1, None), (RIGHT0, RIGHT0, OPP0), (LEFT0, RIGHT1, None), (LEFT1, LEFT1, OPP1)):
-            @pl.when(jnp.logical_and(n >= low, n <= high))
-            def _():
-                total = keep[slot] + drecv[slot]
-                if add is not None:
-                    ring_copy(add).wait_recv()
-                    total = total + rbuf[add - 1]
-                isend[(n - 1) % 4] = total
+        for unit in (OPP0, OPP1, LEFT0):
+            @pl.when(n == unit)
+            def _():
+                isend[place_of(unit)] = keep[slot] + drecv[slot]
+
+        for unit, opp, part in ((RIGHT0, OPP0, 0), (LEFT1, OPP1, 1), (RIGHT1, OPP1, 0)):
+            @pl.when(n == unit)
+            def _():
+                if unit == RIGHT0:
+                    opposite_copy(OPP0, 1).wait_recv()
+                    rest = slice(half_len // 2, half_len)
+                    isend[place_of(LEFT0), rest] += rbuf[OPP0 - 1, rest]
+                else:
+                    for side in range(2):
+                        opposite_copy(unit - LEFT1 + OPP0, side).wait_send()
+                through = slice(part * (half_len // 2), (part + 1) * (half_len // 2))
+                alone = slice((1 - part) * (half_len // 2), (2 - part) * (half_len // 2))
+                isend[place_of(unit), alone] = keep[slot, alone] + drecv[slot, alone]
+                if unit == RIGHT0:
+                    ring_copy(LEFT0).start()
+                opposite_copy(opp, part).wait_recv()
+                isend[place_of(unit), through] = keep[slot, through] + drecv[slot, through] + rbuf[opp - 1, through]
 
         @pl.when(UNITS * layer + n + 2 < UNITS * LAYERS)
         def _():
             pl.semaphore_signal(credit.at[slot], inc=1, device_id={'ep': sib}, device_id_type=MESH)
 
-        @pl.when(jnp.logical_and(n != OWN0, n != OWN1))
-        def _():
-            ring_copy(n).start()
+        for unit in (OPP0, OPP1):
+            @pl.when(n == unit)
+            def _():
+                for side in range(2):
+                    opposite_copy(unit, side).start()
+
+        for unit in (RIGHT0, LEFT1, RIGHT1):
+            @pl.when(n == unit)
+            def _():
+                ring_copy(unit).start()
 
     def unit_step(layer, n):
         @pl.when(n == OPP0)
         def _():
-            shared_expert(layer)
             arrived(OPP0)
             partner_u(OPP0).start()
 
@@ -246,11 +267,16 @@
                 remote(mb.at[n, kk], mb.at[n, kk], mss.at[n, 0], mrs.at[n, kk], sib).wait_recv()
 
         for part, kk in ((0, other), (1, core)):
-            rows = ub[n, kk]
+            picks = []
             for e in range(2):
                 place = mb[n, kk, 2 + e:3 + e, :].astype(jnp.int32)
-                pick = (place == lax.broadcasted_iota(jnp.int32, (rows_half, half_len), 0)).astype(BF16)
-                xb[e, part * rows_half:(part + 1) * rows_half, :] = jnp.dot(pick, rows, preferred_element_type=F32).astype(BF16)
+                picks.append((place == lax.broadcasted_iota(jnp.int32, (rows_half, half_len), 0)).astype(BF16))
+            pick = jnp.concatenate(picks, axis=0)
+            for j in range(n_out):
+                cols = slice(j * CHUNK, (j + 1) * CHUNK)
+                both = jnp.dot(pick, ub[n, kk, :, cols], preferred_element_type=F32).astype(BF16)
+                for e in range(2):
+                    xb[e, part * rows_half:(part + 1) * rows_half, cols] = both[e * rows_half:(e + 1) * rows_half]
 
         def expert_step(e, carry):
             @pl.when(n == OWN0)
@@ -285,9 +311,16 @@
 
             @pl.when(jnp.logical_and(n == LEFT0, e == 0))
             def _():
+                arrived(RIGHT1)
+                ring_u(ub.at[RIGHT1, core], OPP1, left).start()
+                ring_u(ub.at[OWN0, core], RIGHT0, left).start()
+                partner_u(RIGHT1).start()
+
+            @pl.when(jnp.logical_and(n == RIGHT0, e == 0))
+            def _():
                 for slot in range(UNITS):
                     partner_u(slot).wait_send()
-                for slot in range(OPP0, OWN1):
+                for slot in range(LEFT0, OWN1):
                     ring_u(ub.at[slot, core], slot, right).wait_send()
                 for h in range(2):
                     for copy in meta_sends(h):
@@ -329,9 +362,9 @@
         partial_copy(slot).start()
 
     def layer_step(layer, carry):
-        start_for(layer, lambda which: shared_piece(which, 0, 0))
         for e in range(2):
             start_for(layer, lambda which: expert_weights(which, e))
+        start_for(layer, lambda which: shared_piece(which, 0, 0))
 
         def half_step(h, carry):
             @pl.when(layer > 0)
@@ -378,6 +411,7 @@
             return carry
 
         lax.fori_loop(0, UNITS, step, 0)
+        shared_expert(layer)
         merge(layer, OWN1)
         return carry
 
@@ -398,13 +432,13 @@
     specs = [anyspec]
     for params in layers:
         (attn_gain, w_query, w_key, w_value, w_out, moe_gain, w_router, routes, w_gate, w_up, w_down, shared_gate, shared_up, shared_down) = params
-        heads, kv_heads = w_query.shape[1], w_key.shape[1]
-        w_qkv = jnp.concatenate([w.reshape(model_dim, -1) for w in (w_query, w_key, w_value)], axis=1)
+        heads, kv_heads, head_dim = w_query.shape[1], w_key.shape[1], w_query.shape[2]
         operands += [
-            attn_gain.reshape(1, model_dim), w_qkv, w_out.reshape(-1, model_dim), moe_gain.reshape(1, model_dim), w_router.T, jnp.swapaxes(routes, 1, 2),
+            attn_gain, w_query.reshape(model_dim, -1), w_key.reshape(model_dim, -1), w_value.reshape(model_dim, -1), w_out.reshape(-1, model_dim),
+            moe_gain, w_router.T, jnp.swapaxes(routes, 1, 2),
             w_gate, w_up, w_down, shared_gate, shared_up, shared_down,
         ]
-        specs += [vmem, anyspec, anyspec, vmem, vmem, vmem] + [anyspec] * 6
+        specs += [vmem, anyspec, anyspec, anyspec, anyspec, vmem, vmem, vmem] + [anyspec] * 6
     ff = w_gate.shape[2]
     top_k = routes.shape[-1]
     num_experts = w_gate.shape[0] * ep_size
@@ -417,8 +451,8 @@
         in_specs=specs,
         out_specs=vmem,
         scratch_shapes=[
-            pltpu.VMEM(w_qkv.shape, BF16),
-            pltpu.VMEM((heads * w_query.shape[2], model_dim), BF16),
+            pltpu.VMEM((model_dim, (heads + 2 * kv_heads) * head_dim), BF16),
+            pltpu.VMEM((heads * head_dim, model_dim), BF16),
             pltpu.VMEM((UNITS, 2) + block, BF16),
             pltpu.VMEM((UNITS, 2, 8, half_len), F32),
             pltpu.VMEM((2, ep_size, 8, half_len), F32),
@@ -436,10 +470,10 @@
             pltpu.VMEM((2,) + block, F32),
             pltpu.VMEM((4,) + block, F32),
             pltpu.VMEM((6,) + block, F32),
-            dma((3,)), dma((2, 3)), dma((2, 3)),
+            dma((5,)), dma((2, 3)), dma((2, 3)),
             dma((UNITS,)), dma((UNITS,)), dma((UNITS,)), dma((UNITS,)),
             dma((UNITS, 2)), dma((UNITS, 2)),
-            dma((2,)), dma((2,)), dma((UNITS,)), dma((UNITS,)),
+            dma((2,)), dma((2,)), dma((UNITS, 2)), dma((UNITS, 2)),
             pltpu.SemaphoreType.REGULAR((2,)),
         ],
         compiler_params=pltpu.CompilerParams(collective_id=0, has_side_effects=True, vmem_limit_bytes=67043328),

time: 277 us -> 253 us (0.913)
  Pallas kernels: 263 us -> 242 us
  other arithmetic: 3.6 us -> 0 us
    pallas_call x1, Pallas kernels: 263 us -> 242 us  [two_layers(): pl.pallas_call(functools.partial(body, ep_size, heads, kv_heads, top_k, r...]
    reshape x6 -> x3, local copies, waits for them, and re-layouts: 3.89 us -> 8.11 us  [the longest x2 4.86 us: two_layers(): w_value.reshape(model_dim, -1)]
    unnamed x17 -> x5, local copies, waits for them, and re-layouts: 6.17 us -> 2.27 us
    concatenate x2 -> x0, other arithmetic: 3.6 us -> none  [two_layers(): jnp.concatenate([w.reshape(model_dim, -1) for w in (w_query, w_key, w_val...]
where the time goes in v3:
time: 253 us; the launch traced here: 252 us
  Pallas kernels  242 us (96%)
  local copies, waits for them, and re-layouts  10.4 us (4%)
    pallas_call x1, Pallas kernels, two_layers(): pl.pallas_call(functools.partial(body, ep_size, heads, kv_heads, top_k, r...  242 us

profile of v3, /device:TPU:81, one launch (start us, length us, event | category | flops | bytes accessed | tf_op | source)
XLA Modules:
  0.0 252.0 jit_solution(4368360985787471608)
XLA Ops:
  0.0 0.0 copy-start
  0.0 0.0 copy-start.1
  0.0 2.5 copy_bitcast_fusion.4
  2.5 2.4 copy_bitcast_fusion.2
  4.9 0.0 copy-done
  4.9 0.0 copy-done.1
  4.9 3.3 %copy_bitcast_fusion = (bf16[1024,1024]{1,0:T(8,128)(2,1)}, bf16[1024,1024]{1,0:T(8,128)(2,1)}) fusion(bf16[128,8,8,128]{3,2,1,0:T(8,128)(2,1)S(1)} %bitcast.26, bf16[128,8,8,128]{3,2,1,0:T(8,128)(2,1)S(1)} %bitcast.27), kind=kLoop, calls=%fused_computation | loop fusion | bytes 8388608 | tf_op jit(solution)/shard_map/reshape | solution.py:437
  8.1 241.6 %two_layers.1 = bf16[2,256,1024]{2,1,0:T(8,128)(2,1)} custom-call(bf16[2,256,1024]{2,1,0:T(8,128)(2,1)} %x_ref.1, bf16[1024]{0:T(1024)(128)(2,1)} %refs_0_.1, bf16[1024,1024]{1,0:T(8,128)(2,1)} %get-tuple-element.6.refs_1_, bf16[1024,256]{1,0:T(8,128)(2,1)} %get-tuple-element.10.refs_2_, bf16[1024,256]{1,0:T(8,128)(2,1)} %get-tuple-element.9.refs_3_, ...), custom_call_target="tpu_custom_call" | custom-call | tf_op jit(solution)/shard_map/two_layers/pallas_call | solution.py:448
  249.7 2.3 copy.43
Async XLA Ops:
  0.0 4.9 %copy-start = (bf16[1024,8,128]{2,1,0:T(8,128)(2,1)S(1)}, bf16[1024,8,128]{2,1,0:T(8,128)(2,1)}, u32[]{:S(2)}) copy-start(bf16[1024,8,128]{2,1,0:T(8,128)(2,1)} %param.45) | copy-start | bytes 6291460
  0.0 4.9 %copy-start.1 = (bf16[1024,8,128]{2,1,0:T(8,128)(2,1)S(1)}, bf16[1024,8,128]{2,1,0:T(8,128)(2,1)}, u32[]{:S(2)}) copy-start(bf16[1024,8,128]{2,1,0:T(8,128)(2,1)} %param.31) | copy-start | bytes 6291460

commit v4 on v3

--- a/solution.py
+++ b/solution.py
@@ -93,11 +93,13 @@
     x_copy.wait()
     pl.semaphore_wait(barrier, ep_size - 1)
 
-    def ring_u(src, slot, device):
-        return remote(src, ub.at[slot, core], uss.at[slot], urs.at[slot], device)
-
-    def arrived(slot):
-        ring_u(ub.at[slot, core], slot, left).wait_recv()
+    def ring_u(src, slot, part, device):
+        rows = pl.ds(part * (half_len // 2), half_len // 2)
+        return remote(ub.at[src, core, rows], ub.at[slot, core, rows], uss.at[slot, part], urs.at[slot, part], device)
+
+    def arrived(slot, *parts):
+        for part in parts:
+            ring_u(slot, slot, part, left).wait_recv()
 
     def partner_u(slot):
         return remote(ub.at[slot, core], ub.at[slot, core], fs.at[slot], fr.at[slot], sib)
@@ -255,10 +257,10 @@
                 ring_copy(unit).start()
 
     def unit_step(layer, n):
-        @pl.when(n == OPP0)
-        def _():
-            arrived(OPP0)
-            partner_u(OPP0).start()
+        @pl.when(n == OWN0)
+        def _():
+            for copy in expert_weights(0, 0)[:2]:
+                copy.wait()
 
         partner_in(n).wait_recv()
         for part, kk in ((0, other), (1, core)):
@@ -278,23 +280,7 @@
                 for e in range(2):
                     xb[e, part * rows_half:(part + 1) * rows_half, cols] = both[e * rows_half:(e + 1) * rows_half]
 
-        def expert_step(e, carry):
-            @pl.when(n == OWN0)
-            def _():
-                for copy in expert_weights(0, e):
-                    copy.wait()
-
-            @pl.when(jnp.logical_and(n == OPP0, e == 1))
-            def _():
-                arrived(OPP1)
-                partner_u(OPP1).start()
-
-            @pl.when(jnp.logical_and(n == OPP1, e == 1))
-            def _():
-                for slot in (LEFT1, RIGHT0):
-                    arrived(slot)
-                    partner_u(slot).start()
-
+        def up(e):
             rows = xb[e]
             for j in range(n_ff):
                 cols = slice(j * CHUNK, (j + 1) * CHUNK)
@@ -302,40 +288,73 @@
                 up_act = jnp.dot(rows, wu[e, :, cols], preferred_element_type=F32)
                 hb[:, cols] = (jax.nn.silu(gate_act) * up_act).astype(BF16)
 
-            @pl.when(jnp.logical_and(n == OWN0, e == 1))
-            def _():
-                arrived(LEFT0)
-                ring_u(ub.at[LEFT0, core], OPP0, right).start()
-                ring_u(ub.at[OWN1, core], LEFT1, right).start()
-                partner_u(LEFT0).start()
-
-            @pl.when(jnp.logical_and(n == LEFT0, e == 0))
-            def _():
-                arrived(RIGHT1)
-                ring_u(ub.at[RIGHT1, core], OPP1, left).start()
-                ring_u(ub.at[OWN0, core], RIGHT0, left).start()
-                partner_u(RIGHT1).start()
-
-            @pl.when(jnp.logical_and(n == RIGHT0, e == 0))
-            def _():
-                for slot in range(UNITS):
-                    partner_u(slot).wait_send()
-                for slot in range(LEFT0, OWN1):
-                    ring_u(ub.at[slot, core], slot, right).wait_send()
-                for h in range(2):
-                    for copy in meta_sends(h):
-                        copy.wait_send()
-
-            @pl.when(jnp.logical_and(n > 0, e == 0))
-            def _():
-                merge(layer, n - 1)
-
+        def down(e):
             for j in range(n_out):
                 cols = slice(j * CHUNK, (j + 1) * CHUNK)
                 xb[e, :, cols] = jnp.dot(hb[...], wd[e, :, cols], preferred_element_type=F32).astype(BF16)
-            return carry
-
-        lax.fori_loop(0, 2, expert_step, 0)
+
+        up(0)
+
+        @pl.when(n == OWN0)
+        def _():
+            arrived(LEFT0, 0)
+            ring_u(LEFT0, OPP0, 0, right).start()
+            ring_u(OWN1, LEFT1, 0, right).start()
+            arrived(RIGHT0, 1)
+            ring_u(RIGHT0, OPP0, 1, left).start()
+            for copy in expert_weights(0, 0)[2:] + expert_weights(0, 1):
+                copy.wait()
+
+        @pl.when(n == LEFT0)
+        def _():
+            arrived(OPP0, 0, 1)
+            partner_u(OPP0).start()
+
+        @pl.when(n == OPP1)
+        def _():
+            arrived(LEFT1, 1)
+            arrived(RIGHT0, 0)
+            arrived(RIGHT1, 0)
+            for slot in (RIGHT0, LEFT1, RIGHT1):
+                partner_u(slot).start()
+
+        @pl.when(n == RIGHT0)
+        def _():
+            for slot in range(UNITS):
+                partner_u(slot).wait_send()
+            for slot in range(LEFT0, OWN1):
+                for part in range(2):
+                    ring_u(slot, slot, part, right).wait_send()
+            for h in range(2):
+                for copy in meta_sends(h):
+                    copy.wait_send()
+
+        @pl.when(n > 0)
+        def _():
+            merge(layer, n - 1)
+
+        down(0)
+        up(1)
+
+        @pl.when(n == OWN0)
+        def _():
+            arrived(LEFT0, 1)
+            partner_u(LEFT0).start()
+            arrived(RIGHT1, 1)
+            ring_u(RIGHT1, OPP1, 1, left).start()
+            ring_u(OWN0, RIGHT0, 0, left).start()
+            ring_u(OWN1, RIGHT1, 0, left).start()
+
+        @pl.when(n == LEFT0)
+        def _():
+            arrived(LEFT1, 0)
+            ring_u(LEFT1, OPP1, 0, right).start()
+            ring_u(OWN1, LEFT1, 1, right).start()
+
+        @pl.when(n == OPP0)
+        def _():
+            arrived(OPP1, 0, 1)
+            partner_u(OPP1).start()
 
         slot = n % 2
 
@@ -343,6 +362,8 @@
         def _():
             partial_copy(slot).wait_send()
             pl.semaphore_wait(credit.at[slot], 1)
+
+        down(1)
 
         for part, kk in ((0, other), (1, core)):
             columns = jnp.transpose(mb[n, kk])
@@ -381,14 +402,16 @@
 
             @pl.when(h == 0)
             def _():
-                ring_u(ub.at[OWN0, core], LEFT0, right).start()
+                ring_u(OWN0, LEFT0, 0, right).start()
+                ring_u(OWN0, RIGHT0, 1, left).start()
+                ring_u(OWN0, LEFT0, 1, right).start()
                 partner_u(OWN0).start()
                 for copy in meta_sends(0):
                     copy.start()
 
             @pl.when(h == 1)
             def _():
-                ring_u(ub.at[OWN1, core], RIGHT1, left).start()
+                ring_u(OWN1, RIGHT1, 1, left).start()
                 partner_u(OWN1).start()
                 for copy in meta_sends(1):
                     copy.start()
@@ -471,7 +494,7 @@
             pltpu.VMEM((4,) + block, F32),
             pltpu.VMEM((6,) + block, F32),
             dma((5,)), dma((2, 3)), dma((2, 3)),
-            dma((UNITS,)), dma((UNITS,)), dma((UNITS,)), dma((UNITS,)),
+            dma((UNITS,)), dma((UNITS,)), dma((UNITS, 2)), dma((UNITS, 2)),
             dma((UNITS, 2)), dma((UNITS, 2)),
             dma((2,)), dma((2,)), dma((UNITS, 2)), dma((UNITS, 2)),
             pltpu.SemaphoreType.REGULAR((2,)),

time: 253 us -> 244 us (0.964)
  Pallas kernels: 242 us -> 233 us
    pallas_call x1, Pallas kernels: 242 us -> 233 us  [two_layers(): pl.pallas_call(functools.partial(body, ep_size, heads, kv_heads, top_k, r...]
where the time goes in v4:
time: 244 us; the launch traced here: 243 us
  Pallas kernels  233 us (95%)
  local copies, waits for them, and re-layouts  10.4 us (4%)
    pallas_call x1, Pallas kernels, two_layers(): pl.pallas_call(functools.partial(body, ep_size, heads, kv_heads, top_k, r...  233 us

profile of v4, /device:TPU:81, one launch (start us, length us, event | category | flops | bytes accessed | tf_op | source)
XLA Modules:
  0.0 243.5 jit_solution(17573751119631613586)
XLA Ops:
  0.0 0.0 copy-start
  0.0 0.0 copy-start.1
  0.0 2.5 %copy_bitcast_fusion.4 = (bf16[1024,256]{1,0:T(8,128)(2,1)}, bf16[1024,256]{1,0:T(8,128)(2,1)}) fusion(bf16[128,8,2,128]{3,2,1,0:T(2,128)(2,1)} %bitcast.28, bf16[128,8,2,128]{3,2,1,0:T(2,128)(2,1)} %bitcast.29), kind=kLoop, calls=%fused_computation.4 | loop fusion | bytes 2097152 | tf_op jit(solution)/shard_map/reshape | solution.py:460
  2.5 2.4 copy_bitcast_fusion.2
  4.9 0.0 copy-done
  4.9 0.0 copy-done.1
  4.9 3.3 %copy_bitcast_fusion = (bf16[1024,1024]{1,0:T(8,128)(2,1)}, bf16[1024,1024]{1,0:T(8,128)(2,1)}) fusion(bf16[128,8,8,128]{3,2,1,0:T(8,128)(2,1)S(1)} %bitcast.26, bf16[128,8,8,128]{3,2,1,0:T(8,128)(2,1)S(1)} %bitcast.27), kind=kLoop, calls=%fused_computation | loop fusion | bytes 8388608 | tf_op jit(solution)/shard_map/reshape | solution.py:460
  8.1 233.1 %two_layers.1 = bf16[2,256,1024]{2,1,0:T(8,128)(2,1)} custom-call(bf16[2,256,1024]{2,1,0:T(8,128)(2,1)} %x_ref.1, bf16[1024]{0:T(1024)(128)(2,1)} %refs_0_.1, bf16[1024,1024]{1,0:T(8,128)(2,1)} %get-tuple-element.6.refs_1_, bf16[1024,256]{1,0:T(8,128)(2,1)} %get-tuple-element.10.refs_2_, bf16[1024,256]{1,0:T(8,128)(2,1)} %get-tuple-element.9.refs_3_, ...), custom_call_target="tpu_custom_call" | custom-call | tf_op jit(solution)/shard_map/two_layers/pallas_call | solution.py:471
  241.2 2.3 copy.43
Async XLA Ops:
  0.0 4.9 %copy-start = (bf16[1024,8,128]{2,1,0:T(8,128)(2,1)S(1)}, bf16[1024,8,128]{2,1,0:T(8,128)(2,1)}, u32[]{:S(2)}) copy-start(bf16[1024,8,128]{2,1,0:T(8,128)(2,1)} %param.45) | copy-start | bytes 6291460
  0.0 4.9 %copy-start.1 = (bf16[1024,8,128]{2,1,0:T(8,128)(2,1)S(1)}, bf16[1024,8,128]{2,1,0:T(8,128)(2,1)}, u32[]{:S(2)}) copy-start(bf16[1024,8,128]{2,1,0:T(8,128)(2,1)} %param.31) | copy-start | bytes 6291460

commit v5 on v4

--- a/solution.py
+++ b/solution.py
@@ -12,7 +12,7 @@
 F32 = jnp.float32
 BF16 = jnp.bfloat16
 
-OWN0, LEFT0, OPP0, OPP1, RIGHT0, LEFT1, RIGHT1, OWN1 = range(8)
+LEFT0, OPP0, OPP1, RIGHT0, LEFT1, RIGHT1, OWN0, OWN1 = range(8)
 UNITS = 8
 CHUNK = 256
 LAYERS = 2
@@ -30,7 +30,7 @@
     layer_refs = (refs[:14], refs[14:28])
     (
         out_ref,
-        wqkv, wo, ub, mb, ms, wg, wu, wd, sg, su, sd, acc, xb, hb, keep, dsend, drecv, isend, rbuf,
+        qs, ks, vs, wqkv, wo, ub, mb, ms, wg, wu, wd, sg, su, sd, acc, xb, hb, keep, dsend, drecv, isend, rbuf,
         asem, wsem, shsem, fs, fr, uss, urs, mss, mrs, dss, drs, iss, irs, credit,
     ) = refs[28:]
     chips = ep_size // 2
@@ -51,12 +51,26 @@
         return pltpu.make_async_remote_copy(src_ref=src, dst_ref=dst, send_sem=send, recv_sem=recv, device_id={'ep': device}, device_id_type=MESH)
 
     def attention_weights(layer):
-        copies, start = [], 0
-        for i, ref in enumerate(layer_refs[layer][1:4]):
-            copies.append(pltpu.make_async_copy(ref, wqkv.at[:, pl.ds(start, ref.shape[1])], asem.at[i]))
-            start += ref.shape[1]
-        copies.append(pltpu.make_async_copy(layer_refs[layer][4], wo, asem.at[3]))
-        return copies
+        return [
+            pltpu.make_async_copy(ref, target, asem.at[i])
+            for i, (ref, target) in enumerate(zip(layer_refs[layer][1:5], (qs, ks, vs, wo)))
+        ]
+
+    def place_weights():
+        rows = model_dim // 8
+
+        def place(r, carry):
+            at = pl.ds(pl.multiple_of(r * rows, rows), rows)
+            start = 0
+            for staged in (qs, ks, vs):
+                count = staged.shape[1]
+                by_head = jnp.swapaxes(staged[at], 0, 1)
+                for i in range(count):
+                    wqkv[at, start + i * head_dim:start + (i + 1) * head_dim] = by_head[i]
+                start += count * head_dim
+            return carry
+
+        lax.fori_loop(0, 8, place, 0)
 
     def shared_piece(layer, j, slot):
         sg_ref, su_ref, sd_ref = layer_refs[layer][11:14]
@@ -124,21 +138,21 @@
         return remote(dsend.at[slot], drecv.at[slot], dss.at[slot], drs.at[slot], sib)
 
     def place_of(n):
-        return n - 1 - 3 * (n // LEFT1)
+        return n - 3 * (n // LEFT1)
 
     def ring_copy(n):
         device = right if n in (RIGHT0, RIGHT1) else left
-        return remote(isend.at[place_of(n)], rbuf.at[n - 1], iss.at[n, 0], irs.at[n, 0], device)
+        return remote(isend.at[place_of(n)], rbuf.at[n], iss.at[n, 0], irs.at[n, 0], device)
 
     def opposite_copy(n, part):
         rows = pl.ds(part * (half_len // 2), half_len // 2)
-        return remote(isend.at[place_of(n), rows], rbuf.at[n - 1, rows], iss.at[n, part], irs.at[n, part], (right, left)[part])
+        return remote(isend.at[place_of(n), rows], rbuf.at[n, rows], iss.at[n, part], irs.at[n, part], (right, left)[part])
 
     def finish(h):
         from_left, from_right = RIGHT0 + (RIGHT1 - RIGHT0) * h, LEFT0 + (LEFT1 - LEFT0) * h
         for n in (from_left, from_right):
-            remote(rbuf.at[n - 1], rbuf.at[n - 1], iss.at[n, 0], irs.at[n, 0], sib).wait_recv()
-        out_ref[h] = (acc[h] + rbuf[from_left - 1] + rbuf[from_right - 1]).astype(BF16)
+            remote(rbuf.at[n], rbuf.at[n], iss.at[n, 0], irs.at[n, 0], sib).wait_recv()
+        out_ref[h] = (acc[h] + rbuf[from_left] + rbuf[from_right]).astype(BF16)
 
     def per_layer(layer, index):
         return jnp.where(layer == 0, layer_refs[0][index][...].astype(F32), layer_refs[1][index][...].astype(F32))
@@ -166,10 +180,10 @@
             cols = slice(j * CHUNK, (j + 1) * CHUNK)
             projected = jnp.dot(xb[0, 0:half_len, :], wo[:, cols], preferred_element_type=F32)
             acc[h, :, cols] = (out_ref[h, :, cols].astype(F32) + projected).astype(BF16).astype(F32)
-        ub[OWN1 * h, core] = rms_norm(acc[h], gain_of(layer, 5))
+        ub[OWN0 + h, core] = rms_norm(acc[h], gain_of(layer, 5))
 
     def routing_half(layer, h):
-        rows = ub[OWN1 * h, core]
+        rows = ub[OWN0 + h, core]
         router = per_layer(layer, 6).astype(BF16)
         num_experts = router.shape[0]
         logits = lax.dot_general(router, rows, (((1,), (1,)), ((), ())), preferred_element_type=F32)
@@ -188,7 +202,7 @@
             ms[h, dest, 0:2, :] = gates[2 * dest:2 * dest + 2, :]
             ms[h, dest, 2:4, :] = place[2 * dest:2 * dest + 2, :]
             ms[h, dest, 4:8, :] = jnp.zeros((4, half_len), F32)
-        mb[OWN1 * h, core] = ms[h, me]
+        mb[OWN0 + h, core] = ms[h, me]
 
     def shared_expert(layer):
         def shared_step(j, carry):
@@ -197,6 +211,14 @@
             @pl.when(j + 1 < n_ff)
             def _():
                 start_for(layer, lambda which: shared_piece(which, j + 1, (j + 1) % 2))
+
+            @pl.when(j == n_ff // 2 + 1)
+            def _():
+                arrived(LEFT0, 0)
+                ring_u(LEFT0, OPP0, 0, right).start()
+                ring_u(OWN1, LEFT1, 0, right).start()
+                arrived(RIGHT0, 1)
+                ring_u(RIGHT0, OPP0, 1, left).start()
 
             for copy in shared_piece(0, j, slot):
                 copy.wait()
@@ -209,14 +231,20 @@
             return carry
 
         lax.fori_loop(0, n_ff, shared_step, 0)
+        arrived(LEFT0, 1)
+        partner_u(LEFT0).start()
+        arrived(RIGHT1, 1)
+        ring_u(RIGHT1, OPP1, 1, left).start()
+        ring_u(OWN0, RIGHT0, 0, left).start()
+        ring_u(OWN1, RIGHT1, 0, left).start()
 
     def merge(layer, n):
-        slot = n % 2
+        slot = 0
         partial_copy(slot).wait_recv()
 
         @pl.when(jnp.logical_or(n == OWN0, n == OWN1))
         def _():
-            acc[n // OWN1] += keep[slot] + drecv[slot]
+            acc[n % 2] += keep[slot] + drecv[slot]
 
         for unit in (OPP0, OPP1, LEFT0):
             @pl.when(n == unit)
@@ -229,7 +257,7 @@
                 if unit == RIGHT0:
                     opposite_copy(OPP0, 1).wait_recv()
                     rest = slice(half_len // 2, half_len)
-                    isend[place_of(LEFT0), rest] += rbuf[OPP0 - 1, rest]
+                    isend[place_of(LEFT0), rest] += rbuf[OPP0, rest]
                 else:
                     for side in range(2):
                         opposite_copy(unit - LEFT1 + OPP0, side).wait_send()
@@ -239,9 +267,9 @@
                 if unit == RIGHT0:
                     ring_copy(LEFT0).start()
                 opposite_copy(opp, part).wait_recv()
-                isend[place_of(unit), through] = keep[slot, through] + drecv[slot, through] + rbuf[opp - 1, through]
-
-        @pl.when(UNITS * layer + n + 2 < UNITS * LAYERS)
+                isend[place_of(unit), through] = keep[slot, through] + drecv[slot, through] + rbuf[opp, through]
+
+        @pl.when(UNITS * layer + n + 1 < UNITS * LAYERS)
         def _():
             pl.semaphore_signal(credit.at[slot], inc=1, device_id={'ep': sib}, device_id_type=MESH)
 
@@ -257,10 +285,16 @@
                 ring_copy(unit).start()
 
     def unit_step(layer, n):
-        @pl.when(n == OWN0)
+        @pl.when(n == LEFT0)
         def _():
             for copy in expert_weights(0, 0)[:2]:
                 copy.wait()
+
+        @pl.when(n == OPP0)
+        def _():
+            arrived(LEFT1, 0)
+            ring_u(LEFT1, OPP1, 0, right).start()
+            ring_u(OWN1, LEFT1, 1, right).start()
 
         partner_in(n).wait_recv()
         for part, kk in ((0, other), (1, core)):
@@ -280,9 +314,9 @@
                 for e in range(2):
                     xb[e, part * rows_half:(part + 1) * rows_half, cols] = both[e * rows_half:(e + 1) * rows_half]
 
-        def up(e):
+        def up(e, pieces):
             rows = xb[e]
-            for j in range(n_ff):
+            for j in pieces:
                 cols = slice(j * CHUNK, (j + 1) * CHUNK)
                 gate_act = jnp.dot(rows, wg[e, :, cols], preferred_element_type=F32)
                 up_act = jnp.dot(rows, wu[e, :, cols], preferred_element_type=F32)
@@ -293,22 +327,12 @@
                 cols = slice(j * CHUNK, (j + 1) * CHUNK)
                 xb[e, :, cols] = jnp.dot(hb[...], wd[e, :, cols], preferred_element_type=F32).astype(BF16)
 
-        up(0)
-
-        @pl.when(n == OWN0)
-        def _():
-            arrived(LEFT0, 0)
-            ring_u(LEFT0, OPP0, 0, right).start()
-            ring_u(OWN1, LEFT1, 0, right).start()
-            arrived(RIGHT0, 1)
-            ring_u(RIGHT0, OPP0, 1, left).start()
+        up(0, range(n_ff // 2 + 1))
+
+        @pl.when(n == LEFT0)
+        def _():
             for copy in expert_weights(0, 0)[2:] + expert_weights(0, 1):
                 copy.wait()
-
-        @pl.when(n == LEFT0)
-        def _():
-            arrived(OPP0, 0, 1)
-            partner_u(OPP0).start()
 
         @pl.when(n == OPP1)
         def _():
@@ -322,7 +346,7 @@
         def _():
             for slot in range(UNITS):
                 partner_u(slot).wait_send()
-            for slot in range(LEFT0, OWN1):
+            for slot in range(LEFT0, OWN0):
                 for part in range(2):
                     ring_u(slot, slot, part, right).wait_send()
             for h in range(2):
@@ -333,32 +357,23 @@
         def _():
             merge(layer, n - 1)
 
+        up(0, range(n_ff // 2 + 1, n_ff))
         down(0)
-        up(1)
-
-        @pl.when(n == OWN0)
-        def _():
-            arrived(LEFT0, 1)
-            partner_u(LEFT0).start()
-            arrived(RIGHT1, 1)
-            ring_u(RIGHT1, OPP1, 1, left).start()
-            ring_u(OWN0, RIGHT0, 0, left).start()
-            ring_u(OWN1, RIGHT1, 0, left).start()
+        up(1, range(n_ff))
 
         @pl.when(n == LEFT0)
         def _():
-            arrived(LEFT1, 0)
-            ring_u(LEFT1, OPP1, 0, right).start()
-            ring_u(OWN1, LEFT1, 1, right).start()
+            arrived(OPP0, 0, 1)
+            partner_u(OPP0).start()
 
         @pl.when(n == OPP0)
         def _():
             arrived(OPP1, 0, 1)
             partner_u(OPP1).start()
 
-        slot = n % 2
-
-        @pl.when(UNITS * layer + n >= 2)
+        slot = 0
+
+        @pl.when(UNITS * layer + n >= 1)
         def _():
             partial_copy(slot).wait_send()
             pl.semaphore_wait(credit.at[slot], 1)
@@ -383,9 +398,9 @@
         partial_copy(slot).start()
 
     def layer_step(layer, carry):
+        start_for(layer, lambda which: shared_piece(which, 0, 0))
         for e in range(2):
             start_for(layer, lambda which: expert_weights(which, e))
-        start_for(layer, lambda which: shared_piece(which, 0, 0))
 
         def half_step(h, carry):
             @pl.when(layer > 0)
@@ -396,6 +411,7 @@
             def _():
                 for copy in attention_weights(0):
                     copy.wait()
+                place_weights()
 
             attention_half(layer, h)
             routing_half(layer, h)
@@ -433,8 +449,8 @@
             unit_step(layer, n)
             return carry
 
+        shared_expert(layer)
         lax.fori_loop(0, UNITS, step, 0)
-        shared_expert(layer)
         merge(layer, OWN1)
         return carry
 
@@ -443,8 +459,7 @@
         finish(h)
     for n in (RIGHT0, LEFT0, RIGHT1, LEFT1):
         ring_copy(n).wait_send()
-    for slot in range(2):
-        partial_copy(slot).wait_send()
+    partial_copy(0).wait_send()
 
 
 def two_layers(tokens, layers, ep_size):
@@ -457,7 +472,7 @@
         (attn_gain, w_query, w_key, w_value, w_out, moe_gain, w_router, routes, w_gate, w_up, w_down, shared_gate, shared_up, shared_down) = params
         heads, kv_heads, head_dim = w_query.shape[1], w_key.shape[1], w_query.shape[2]
         operands += [
-            attn_gain, w_query.reshape(model_dim, -1), w_key.reshape(model_dim, -1), w_value.reshape(model_dim, -1), w_out.reshape(-1, model_dim),
+            attn_gain, w_query, w_key, w_value, w_out.reshape(-1, model_dim),
             moe_gain, w_router.T, jnp.swapaxes(routes, 1, 2),
             w_gate, w_up, w_down, shared_gate, shared_up, shared_down,
         ]
@@ -474,6 +489,9 @@
         in_specs=specs,
         out_specs=vmem,
         scratch_shapes=[
+            pltpu.VMEM(w_query.shape, BF16),
+            pltpu.VMEM(w_key.shape, BF16),
+            pltpu.VMEM(w_value.shape, BF16),
             pltpu.VMEM((model_dim, (heads + 2 * kv_heads) * head_dim), BF16),
             pltpu.VMEM((heads * head_dim, model_dim), BF16),
             pltpu.VMEM((UNITS, 2) + block, BF16),
@@ -488,16 +506,16 @@
             pltpu.VMEM((2,) + block, F32),
             pltpu.VMEM((2, 2 * rows_half, model_dim), BF16),
             pltpu.VMEM((2 * rows_half, ff), BF16),
-            pltpu.VMEM((2,) + block, F32),
-            pltpu.VMEM((2,) + block, F32),
-            pltpu.VMEM((2,) + block, F32),
+            pltpu.VMEM((1,) + block, F32),
+            pltpu.VMEM((1,) + block, F32),
+            pltpu.VMEM((1,) + block, F32),
             pltpu.VMEM((4,) + block, F32),
             pltpu.VMEM((6,) + block, F32),
             dma((5,)), dma((2, 3)), dma((2, 3)),
             dma((UNITS,)), dma((UNITS,)), dma((UNITS, 2)), dma((UNITS, 2)),
             dma((UNITS, 2)), dma((UNITS, 2)),
-            dma((2,)), dma((2,)), dma((UNITS, 2)), dma((UNITS, 2)),
-            pltpu.SemaphoreType.REGULAR((2,)),
+            dma((1,)), dma((1,)), dma((UNITS, 2)), dma((UNITS, 2)),
+            pltpu.SemaphoreType.REGULAR((1,)),
         ],
         compiler_params=pltpu.CompilerParams(collective_id=0, has_side_effects=True, vmem_limit_bytes=67043328),
         name='two_layers',

time: 244 us -> 234 us (0.959)
  local copies, waits for them, and re-layouts: 10.4 us -> 2.26 us
    reshape x3 -> x0, local copies, waits for them, and re-layouts: 8.11 us -> none  [the longest x2 4.86 us: two_layers(): w_value.reshape(model_dim, -1)]
where the time goes in v5:
time: 234 us
  Pallas kernels  231 us (99%)
    pallas_call x1, Pallas kernels, two_layers(): pl.pallas_call(functools.partial(body, ep_size, heads, kv_heads, top_k, r...  231 us

profile of v5, /device:TPU:81, one launch (start us, length us, event | category | flops | bytes accessed | tf_op | source)
XLA Modules:
  0.0 233.6 jit_solution(815830827481881255)
XLA Ops:
  0.0 231.3 %two_layers.1 = bf16[2,256,1024]{2,1,0:T(8,128)(2,1)} custom-call(bf16[2,256,1024]{2,1,0:T(8,128)(2,1)} %x_ref.1, bf16[1024]{0:T(1024)(128)(2,1)} %refs_0_.1, bf16[1024,8,128]{2,1,0:T(8,128)(2,1)} %refs_1_.1, bf16[1024,2,128]{2,1,0:T(2,128)(2,1)} %refs_2_.1, bf16[1024,2,128]{2,1,0:T(2,128)(2,1)} %refs_3_.1, bf16[1024,1024]{1,0:T(8,128)(2,1)} %bitcast.6, ...), custom_call_target="tpu_custom_call" | custom-call | tf_op jit(solution)/shard_map/two_layers/pallas_call | solution.py:486
  231.3 2.3 copy.31

commit v6 on v5

--- a/solution.py
+++ b/solution.py
@@ -409,9 +409,11 @@
 
             @pl.when(h == 0)
             def _():
-                for copy in attention_weights(0):
+                *projections, out_weights = attention_weights(0)
+                for copy in projections:
                     copy.wait()
                 place_weights()
+                out_weights.wait()
 
             attention_half(layer, h)
             routing_half(layer, h)
@@ -485,7 +487,7 @@
     dma = pltpu.SemaphoreType.DMA
     return pl.pallas_call(
         functools.partial(body, ep_size, heads, kv_heads, top_k, rows_half),
-        out_shape=jax.ShapeDtypeStruct(tokens.shape, BF16),
+        out_shape=pltpu.VMEM(tokens.shape, BF16),
         in_specs=specs,
         out_specs=vmem,
         scratch_shapes=[
@@ -517,7 +519,7 @@
             dma((1,)), dma((1,)), dma((UNITS, 2)), dma((UNITS, 2)),
             pltpu.SemaphoreType.REGULAR((1,)),
         ],
-        compiler_params=pltpu.CompilerParams(collective_id=0, has_side_effects=True, vmem_limit_bytes=67043328),
+        compiler_params=pltpu.CompilerParams(collective_id=0, has_side_effects=True, vmem_limit_bytes=62 * 2**20),
         name='two_layers',
     )(*operands)
 

time: 234 us -> 231 us (0.987)
  no operation moved by 1% of the time
where the time goes in v6:
time: 231 us
  Pallas kernels  230 us (100%)
    pallas_call x1, Pallas kernels, two_layers(): pl.pallas_call(functools.partial(body, ep_size, heads, kv_heads, top_k, r...  230 us

profile of v6, /device:TPU:81, one launch (start us, length us, event | category | flops | bytes accessed | tf_op | source)
XLA Modules:
  0.0 230.5 jit_solution(16844110825079934558)
XLA Ops:
  0.0 229.5 %two_layers.1 = bf16[2,256,1024]{2,1,0:T(8,128)(2,1)S(1)} custom-call(bf16[2,256,1024]{2,1,0:T(8,128)(2,1)} %x_ref.1, bf16[1024]{0:T(1024)(128)(2,1)} %refs_0_.1, bf16[1024,8,128]{2,1,0:T(8,128)(2,1)} %refs_1_.1, bf16[1024,2,128]{2,1,0:T(2,128)(2,1)} %refs_2_.1, bf16[1024,2,128]{2,1,0:T(2,128)(2,1)} %refs_3_.1, bf16[1024,1024]{1,0:T(8,128)(2,1)} %bitcast.6, ...), custom_call_target="tpu_custom_call" | custom-call | tf_op jit(solution)/shard_map/two_layers/pallas_call | solution.py:488
  229.5 1.0 copy.31

commit v7 on v6

--- a/solution.py
+++ b/solution.py
@@ -70,7 +70,7 @@
                 start += count * head_dim
             return carry
 
-        lax.fori_loop(0, 8, place, 0)
+        lax.fori_loop(0, 8, place, 0, unroll=True)
 
     def shared_piece(layer, j, slot):
         sg_ref, su_ref, sd_ref = layer_refs[layer][11:14]
@@ -115,11 +115,18 @@
         for part in parts:
             ring_u(slot, slot, part, left).wait_recv()
 
-    def partner_u(slot):
-        return remote(ub.at[slot, core], ub.at[slot, core], fs.at[slot], fr.at[slot], sib)
-
-    def partner_in(slot):
-        return remote(ub.at[slot, other], ub.at[slot, other], fs.at[slot], fr.at[slot], sib)
+    def partner_u(slot, part):
+        rows = pl.ds(part * (half_len // 2), half_len // 2)
+        return remote(ub.at[slot, core, rows], ub.at[slot, core, rows], fs.at[slot, part], fr.at[slot, part], sib)
+
+    def hand_over(slot, *parts):
+        for part in parts:
+            partner_u(slot, part).start()
+
+    def handed(slot):
+        for part in range(2):
+            rows = pl.ds(part * (half_len // 2), half_len // 2)
+            remote(ub.at[slot, other, rows], ub.at[slot, other, rows], fs.at[slot, part], fr.at[slot, part], sib).wait_recv()
 
     hops = ((0, (OWN0, OWN1)), (1, (LEFT0, LEFT1)), (2, (OPP0, OPP1)), (3, (RIGHT0, RIGHT1)))
 
@@ -217,6 +224,7 @@
                 arrived(LEFT0, 0)
                 ring_u(LEFT0, OPP0, 0, right).start()
                 ring_u(OWN1, LEFT1, 0, right).start()
+                hand_over(LEFT0, 0)
                 arrived(RIGHT0, 1)
                 ring_u(RIGHT0, OPP0, 1, left).start()
 
@@ -232,7 +240,7 @@
 
         lax.fori_loop(0, n_ff, shared_step, 0)
         arrived(LEFT0, 1)
-        partner_u(LEFT0).start()
+        hand_over(LEFT0, 1)
         arrived(RIGHT1, 1)
         ring_u(RIGHT1, OPP1, 1, left).start()
         ring_u(OWN0, RIGHT0, 0, left).start()
@@ -296,13 +304,14 @@
             ring_u(LEFT1, OPP1, 0, right).start()
             ring_u(OWN1, LEFT1, 1, right).start()
 
-        partner_in(n).wait_recv()
-        for part, kk in ((0, other), (1, core)):
+        for part, kk in ((1, core), (0, other)):
+            if part == 0:
+                handed(n)
+
             @pl.when(jnp.logical_or(jnp.logical_and(n != OWN0, n != OWN1), kk != core))
             def _():
                 remote(mb.at[n, kk], mb.at[n, kk], mss.at[n, 0], mrs.at[n, kk], sib).wait_recv()
 
-        for part, kk in ((0, other), (1, core)):
             picks = []
             for e in range(2):
                 place = mb[n, kk, 2 + e:3 + e, :].astype(jnp.int32)
@@ -340,12 +349,13 @@
             arrived(RIGHT0, 0)
             arrived(RIGHT1, 0)
             for slot in (RIGHT0, LEFT1, RIGHT1):
-                partner_u(slot).start()
+                hand_over(slot, 0, 1)
 
         @pl.when(n == RIGHT0)
         def _():
             for slot in range(UNITS):
-                partner_u(slot).wait_send()
+                for part in range(2):
+                    partner_u(slot, part).wait_send()
             for slot in range(LEFT0, OWN0):
                 for part in range(2):
                     ring_u(slot, slot, part, right).wait_send()
@@ -364,12 +374,12 @@
         @pl.when(n == LEFT0)
         def _():
             arrived(OPP0, 0, 1)
-            partner_u(OPP0).start()
+            hand_over(OPP0, 0, 1)
 
         @pl.when(n == OPP0)
         def _():
             arrived(OPP1, 0, 1)
-            partner_u(OPP1).start()
+            hand_over(OPP1, 0, 1)
 
         slot = 0
 
@@ -423,14 +433,14 @@
                 ring_u(OWN0, LEFT0, 0, right).start()
                 ring_u(OWN0, RIGHT0, 1, left).start()
                 ring_u(OWN0, LEFT0, 1, right).start()
-                partner_u(OWN0).start()
+                hand_over(OWN0, 0, 1)
                 for copy in meta_sends(0):
                     copy.start()
 
             @pl.when(h == 1)
             def _():
                 ring_u(OWN1, RIGHT1, 1, left).start()
-                partner_u(OWN1).start()
+                hand_over(OWN1, 0, 1)
                 for copy in meta_sends(1):
                     copy.start()
             return carry
@@ -514,7 +524,7 @@
             pltpu.VMEM((4,) + block, F32),
             pltpu.VMEM((6,) + block, F32),
             dma((5,)), dma((2, 3)), dma((2, 3)),
-            dma((UNITS,)), dma((UNITS,)), dma((UNITS, 2)), dma((UNITS, 2)),
+            dma((UNITS, 2)), dma((UNITS, 2)), dma((UNITS, 2)), dma((UNITS, 2)),
             dma((UNITS, 2)), dma((UNITS, 2)),
             dma((1,)), dma((1,)), dma((UNITS, 2)), dma((UNITS, 2)),
             pltpu.SemaphoreType.REGULAR((1,)),

time: 231 us -> 230 us (level)
  no operation moved by 1% of the time
where the time goes in v7:
time: 230 us
  Pallas kernels  229 us (100%)
    pallas_call x1, Pallas kernels, two_layers(): pl.pallas_call(functools.partial(body, ep_size, heads, kv_heads, top_k, r...  229 us

profile of v7, /device:TPU:81, one launch (start us, length us, event | category | flops | bytes accessed | tf_op | source)
XLA Modules:
  0.0 229.9 jit_solution(4523252274100703312)
XLA Ops:
  0.0 228.9 %two_layers.1 = bf16[2,256,1024]{2,1,0:T(8,128)(2,1)S(1)} custom-call(bf16[2,256,1024]{2,1,0:T(8,128)(2,1)} %x_ref.1, bf16[1024]{0:T(1024)(128)(2,1)} %refs_0_.1, bf16[1024,8,128]{2,1,0:T(8,128)(2,1)} %refs_1_.1, bf16[1024,2,128]{2,1,0:T(2,128)(2,1)} %refs_2_.1, bf16[1024,2,128]{2,1,0:T(2,128)(2,1)} %refs_3_.1, bf16[1024,1024]{1,0:T(8,128)(2,1)} %bitcast.6, ...), custom_call_target="tpu_custom_call" | custom-call | tf_op jit(solution)/shard_map/two_layers/pallas_call | solution.py:498
  228.9 1.0 copy.31
